TPU v7x, 256 devices: a whole 4x4x8 slice. The times are simulated.
256 devices in a mesh: head: 4 (over y_hi, core), seq: 64 (over x, y_lo, z).
Axes of the slice: x: 4, y: 4 (y_hi: 2, y_lo: 2; y = y_hi * 2 + y_lo), z: 8, core: 2. Of those that a mesh axis runs over, the one named last changes fastest.
Arguments:
- keys: bfloat16 [12288, 2560], P('seq', 'head'), may hold values from -6 to 6
- values: bfloat16 [12288, 2560], P('seq', 'head'), may hold values from -6 to 6
- queries: bfloat16 [12288, 2560], P('seq', 'head'), may hold values from -6 to 6
- step_size: float32 [12288, 2], P('seq'), may hold values from 7.564421e-05 to 0.0007564421
- gate_weight: bfloat16 [1280, 3072], P('seq', 'head'), may hold values from -1 to 1
- up_weight: bfloat16 [1280, 3072], P('seq', 'head'), may hold values from -1 to 1
- down_weight: bfloat16 [1280, 3072], P('seq', 'head'), may hold values from -1 to 1
Outputs:
- mixed: bfloat16 [12288, 2560], P('seq', 'head')
All inputs are finite; a program needn't handle non-finite values.
Results may differ from a plain program's by a relative error of at most 0.0066.
Values may be sent and summed in bfloat16 or wider, within the bound.
A program may use at most 128 MiB of HBM per device.

v0:
```python
import jax
import jax.numpy as jnp
from jax import lax
from jax.sharding import Mesh
from jax.sharding import PartitionSpec as P

SEQ = ("seq_0", "seq_1", "seq_2")


epsilon = 1e-06


def swapped(value, axis, stride):
    mask = 2**stride
    pairs = [(source, source ^ mask) for source in range(lax.axis_size(axis))]
    return lax.ppermute(value, axis, pairs)


def in_one_piece(arrays, axis, dim, along):
    both = jnp.concatenate(arrays, axis=along)
    whole, at, done = (lax.all_gather(both, axis, axis=dim, tiled=True), 0, [])
    for a in arrays:
        done.append(lax.slice_in_dim(whole, at, at + a.shape[along], axis=along))
        at += a.shape[along]
    return tuple(done)


def split_up(value, dim, peers):
    before, after = (value.shape[:dim], value.shape[dim + 1 :])
    return jnp.moveaxis(value.reshape(*before, peers, -1, *after), dim, 0)


def cut_rows(length, count):
    step = length // count
    if step >= 8:
        step -= step % 8
    return [step * k for k in range(1, count)]


def reduced_to_own(pieces, axes, order):
    dims = [lax.axis_size(a) for a in axes]
    pieces = pieces.reshape(*dims, *pieces.shape[1:])
    pieces = pieces.transpose(*order, *range(len(axes), pieces.ndim))
    pieces = pieces.reshape(-1, *pieces.shape[len(axes) :])
    for k in order:
        pieces = lax.psum_scatter(pieces, axes[k], scatter_dimension=0, tiled=True)
    return pieces[0]


def spread_scatter(value, axes, dim):
    pieces = split_up(value, dim, lax.axis_size(axes))
    split_at = max(range(1, max(2, pieces.ndim - 1)), key=lambda d: pieces.shape[d])
    count, done = (len(axes), [])
    for initial, slab in enumerate(
        jnp.split(pieces, cut_rows(pieces.shape[split_at], count), axis=split_at)
    ):
        if slab.size:
            order = [(initial + k) % count for k in range(count)]
            done.append(reduced_to_own(slab, axes, order))
    return jnp.concatenate(done, axis=split_at - 1)


def silu_slope(values_in):
    sigma = jax.nn.sigmoid(values_in)
    return sigma * (1.0 + values_in * (1.0 - sigma))


def square_sums(matrix, axis_id):
    return jnp.sum(jnp.square(matrix.astype(jnp.float32)), axis=axis_id)


def join_halves(own_part, other_part, half_index):
    first_half = jnp.where(half_index == 0, own_part, other_part)
    second_half = jnp.where(half_index == 0, other_part, own_part)
    return jnp.concatenate([first_half, second_half], axis=1)


def contract_rows(left, right):
    return lax.dot_general(
        left, right, (((0,), (0,)), ((), ())), preferred_element_type=jnp.float32
    )


def contract_cols(left, right):
    return lax.dot_general(
        left, right, (((1,), (1,)), ((), ())), preferred_element_type=jnp.float32
    )


def body(keys, values, queries, step_size, gate_weight, up_weight, down_weight):
    position = lax.axis_index("head")
    half_index = position % 2
    head_index = position // 2
    other_keys, other_values = swapped((keys, values), "head", 0)
    key_full = join_halves(keys, other_keys, half_index)
    value_full = join_halves(values, other_values, half_index)
    rates = lax.dynamic_slice_in_dim(step_size, head_index, 1, 1)
    full_gate, full_up, full_down = in_one_piece((gate_weight, up_weight, down_weight), SEQ, 0, 1)
    gate_act = jnp.dot(key_full, full_gate, preferred_element_type=jnp.float32)
    up_act = jnp.dot(key_full, full_up, preferred_element_type=jnp.float32)
    silu_gate = jax.nn.silu(gate_act)
    hidden = (silu_gate * up_act).astype(jnp.bfloat16)
    outgrad = (-(rates * value_full.astype(jnp.float32))).astype(jnp.bfloat16)
    hidden_grad = jnp.dot(outgrad, full_down, preferred_element_type=jnp.float32)
    gate_grad = (hidden_grad * up_act * silu_slope(gate_act)).astype(jnp.bfloat16)
    up_grad = (hidden_grad * silu_gate).astype(jnp.bfloat16)
    old_gate_sums = square_sums(full_gate, 0)
    old_up_sums = square_sums(full_up, 0)
    old_down_sums = square_sums(full_down, 0)
    feature_count = key_full.shape[1]
    unit_count = gate_weight.shape[1]
    shard_count = lax.axis_size(SEQ)
    unit_share = unit_count // shard_count
    own_first = lax.axis_index(SEQ) * unit_share
    gradients = spread_scatter(
        jnp.concatenate(
            [
                contract_rows(gate_grad, key_full),
                contract_rows(up_grad, key_full),
                contract_rows(hidden, outgrad),
            ],
            axis=1,
        ),
        SEQ,
        0,
    )
    old_gate_units = lax.dynamic_slice_in_dim(full_gate, own_first, unit_share, 1).T
    old_up_units = lax.dynamic_slice_in_dim(full_up, own_first, unit_share, 1).T
    old_down_units = lax.dynamic_slice_in_dim(full_down, own_first, unit_share, 1).T
    new_gate = (old_gate_units.astype(jnp.float32) - gradients[:, :feature_count]).astype(
        jnp.bfloat16
    )
    new_up = (
        old_up_units.astype(jnp.float32) - gradients[:, feature_count : 2 * feature_count]
    ).astype(jnp.bfloat16)
    new_down = (old_down_units.astype(jnp.float32) - gradients[:, 2 * feature_count :]).astype(
        jnp.bfloat16
    )
    other_queries = swapped(queries, "head", 0)
    query_full = join_halves(queries, other_queries, half_index)
    pieces = in_one_piece((new_gate, new_up, new_down), SEQ, 0, 1)
    ratio_gate = jnp.sqrt((old_gate_sums + epsilon) / (square_sums(pieces[0], 1) + epsilon))
    ratio_up = jnp.sqrt((old_up_sums + epsilon) / (square_sums(pieces[1], 1) + epsilon))
    ratio_down = jnp.sqrt((old_down_sums + epsilon) / (square_sums(pieces[2], 1) + epsilon))
    query_gate = contract_cols(query_full, pieces[0]) * ratio_gate
    query_up = contract_cols(query_full, pieces[1]) * ratio_up
    query_hidden = (jax.nn.silu(query_gate) * query_up * ratio_down).astype(jnp.bfloat16)
    partial_sums = jnp.dot(query_hidden, pieces[2], preferred_element_type=jnp.float32)
    half_width = feature_count // 2
    kept_sums = lax.dynamic_slice_in_dim(partial_sums, half_index * half_width, half_width, 1)
    sent_sums = lax.dynamic_slice_in_dim(partial_sums, (1 - half_index) * half_width, half_width, 1)
    received = swapped(sent_sums, "head", 0)
    return (kept_sums + received).astype(jnp.bfloat16)


def solution(mesh):
    finer = Mesh(
        mesh.devices.reshape(mesh.shape["head"], 4, 2, 8), ("head", "seq_0", "seq_1", "seq_2")
    )
    placed = (
        P(SEQ, "head"),
        P(SEQ, "head"),
        P(SEQ, "head"),
        P(SEQ, None),
        P(SEQ, "head"),
        P(SEQ, "head"),
        P(SEQ, "head"),
    )
    return jax.shard_map(
        body, mesh=finer, in_specs=placed, out_specs=P(SEQ, "head"), check_vma=False
    )
```

profile of v0, /device:TPU:1, one launch (start us, length us, event | category | flops | bytes accessed | tf_op | source)
XLA Modules:
  0.0 1187.2 jit_solution(18168465409778158775)
XLA Ops:
  6.5 1.5 maximum_bitcast_fusion.1
  8.1 3.3 collective-permute-start.1
  11.5 1.2 collective-permute-done.1
  12.7 1.0 broadcast_select_fusion.3
  13.7 1.0 broadcast_select_fusion.1
  14.7 264.1 %all-gather.5.cloned.1.call-done = bf16[64,20,2304]{2,1,0:T(8,128)(2,1)} async-done(((bf16[1,20,2304]{2,1,0:T(8,128)(2,1)}), bf16[64,20,2304]{2,1,0:T(8,128)(2,1)}) %all-gather.5.cloned.1.call-update) | async-done | bytes 5898256 | tf_op jit(solution)/shard_map/all_gather | solution.py:21
  278.9 9.4 reshape.45
  288.3 2.1 fusion.36
  290.4 2.1 fusion.37
  292.5 2.2 fusion.38
  294.7 0.8 fusion.18
  295.5 0.9 fusion.17
  296.4 0.9 fusion.19
  297.3 4.7 pad_maximum_fusion
  302.0 13.3 %reshape.39 = f32[64,12,3840]{2,1,0:T(8,128)} reshape(f32[768,3840]{1,0:T(8,128)} %pad_maximum_fusion) | data formatting | bytes 23592960 | tf_op jit(solution)/shard_map/reshape | solution.py:30
  315.3 12.7 %fusion.42 = (f32[64,4,3840]{2,1,0:T(4,128)}, f32[64,4,3840]{2,1,0:T(4,128)}, f32[64,4,3840]{2,1,0:T(4,128)}) fusion(f32[64,12,3840]{2,1,0:T(8,128)} %reshape.39), kind=kLoop, calls=%fused_computation.73 | loop fusion | bytes 23592960 | tf_op jit(solution)/shard_map/split | solution.py:55
  329.8 4.6 copy.36
  334.4 127.5 %all-reduce.18.cloned.1.call-done = f32[64,4,3840]{2,1,0:T(4,128)} async-done(((f32[64,4,3840]{2,1,0:T(4,128)}), f32[64,4,3840]{2,1,0:T(4,128)}) %all-reduce.18.cloned.1.call-update) | async-done | bytes 3932176
  461.8 2.2 constant_dynamic-slice_fusion.5
  466.2 4.4 copy.37
  470.6 129.2 %all-reduce.26.cloned.1.call-done = (f32[64,4,3840]{2,1,0:T(4,128)}, f32[16,4,3840]{2,1,0:T(4,128)}) async-done(((f32[64,4,3840]{2,1,0:T(4,128)}, f32[16,4,3840]{2,1,0:T(4,128)}), (f32[64,4,3840]{2,1,0:T(4,128)}, f32[16,4,3840]{2,1,0:T(4,128)})) %all-reduce.26.cloned.1.call-update) | async-done | bytes 4915216
  599.8 3.1 constant_dynamic-slice_fusion.3
  602.9 0.8 constant_dynamic-slice_fusion.4
  606.2 149.3 %all-reduce.22.cloned.1.call-done = (f32[64,4,3840]{2,1,0:T(4,128)}, f32[32,4,3840]{2,1,0:T(4,128)}, f32[8,4,3840]{2,1,0:T(4,128)}) async-done(((f32[64,4,3840]{2,1,0:T(4,128)}, f32[32,4,3840]{2,1,0:T(4,128)}, f32[8,4,3840]{2,1,0:T(4,128)}), (f32[64,4,3840]{2,1,0:T(4,128)}, f32[32,4,3840]{2,1,0:T(4,128)}, f32[8,4,3840]{2,1,0:T(4,128)})) %all-reduce.22.cloned.1.call-update) | async-done | bytes 6389776
  755.6 1.8 constant_dynamic-slice_fusion.1
  757.4 1.7 constant_dynamic-slice_fusion.2
  759.1 5.4 fusion.43
  764.5 2.7 copy.38
  767.2 4.0 copy.39
  771.2 4.0 copy.40
  775.2 1.5 dynamic-slice_bitcast_fusion.2
  776.7 28.6 %all-reduce.24.cloned.1.call-done = (f32[8,4,3840]{2,1,0:T(4,128)}, f32[4,4,3840]{2,1,0:T(4,128)}) async-done(((f32[8,4,3840]{2,1,0:T(4,128)}, f32[4,4,3840]{2,1,0:T(4,128)}), (f32[8,4,3840]{2,1,0:T(4,128)}, f32[4,4,3840]{2,1,0:T(4,128)})) %all-reduce.24.cloned.1.call-update) | async-done | bytes 737296
  805.2 1.6 constant_dynamic-slice_fusion
  806.9 1.4 dynamic-slice_bitcast_fusion.1
  808.2 35.2 %all-reduce.20.cloned.1.call-done = f32[2,4,3840]{2,1,0:T(4,128)} async-done(((f32[2,4,3840]{2,1,0:T(4,128)}), f32[2,4,3840]{2,1,0:T(4,128)}) %all-reduce.20.cloned.1.call-update) | async-done | bytes 122896
  843.5 1.5 dynamic-slice_bitcast_fusion
  845.0 0.9 fusion.28
  846.7 1.3 collective-permute-start
  848.0 1.1 collective-permute-done
  849.2 2.0 multiply_reduce_fusion.1
  852.1 264.4 %all-gather.7.cloned.1.call-done = bf16[64,12,3840]{2,1,0:T(8,128)(2,1)} async-done(((bf16[1,12,3840]{2,1,0:T(8,128)(2,1)}), bf16[64,12,3840]{2,1,0:T(8,128)(2,1)}) %all-gather.7.cloned.1.call-update) | async-done | bytes 5898256 | tf_op jit(solution)/shard_map/all_gather | solution.py:21
  1116.5 9.6 reshape.47
  1126.1 4.0 multiply_reduce_fusion.2
  1130.1 2.4 fusion.6
  1132.5 3.7 fusion
  1136.2 41.9 %collective-permute-start.3 = (f32[192,640]{1,0:T(8,128)S(1)}, f32[192,640]{1,0:T(8,128)S(1)}, u32[]{:S(2)}, u32[]{:S(2)}) collective-permute-start(f32[192,640]{1,0:T(8,128)S(1)} %constant_dynamic-slice_fusion.6), channel_id=1, source_target_pairs={{0,64},{64,0},{128,192},{192,128},{1,65},{65,1},{129,193},{193,129... | collective-permute-start | bytes 1474568 | tf_op jit(solution)/shard_map/ppermute | solution.py:16
  1178.1 1.5 collective-permute-done.3
  1179.6 0.8 add_convert_fusion
  (44 shorter events, 4.7 us)
Async XLA Ops:
  6.5 4.9 copy-start
  6.5 272.3 %all-gather.5.cloned.1.call-start = ((), (), s32[]{:S(2)}) async-start(), calls=%async_computation | async-start | bytes 7188480 | tf_op jit(solution)/shard_map/all_gather | solution.py:21
  8.0 453.8 %all-reduce.18.cloned.1.call-start = ((), (), s32[]{:S(2)}) async-start(), calls=%async_computation.2 | async-start | bytes 7864320
  8.1 4.6 collective-permute-start.1
  11.4 2.4 collective-permute-start.2
  328.0 0.7 copy-start.7
  328.0 271.8 %all-reduce.26.cloned.1.call-start = ((), (), s32[]{:S(2)}) async-start(), calls=%async_computation.6 | async-start | bytes 9830400
  334.4 129.7 %copy-start.6 = (u32[256]{0:T(256)S(1)}, u32[256]{0:T(256)}, u32[]{:S(2)}) copy-start(u32[256]{0:T(256)} %constant.74) | copy-start | bytes 3076
  464.1 291.5 %all-reduce.22.cloned.1.call-start = ((), (), s32[]{:S(2)}) async-start(), calls=%async_computation.4 | async-start | bytes 12779520
  599.8 3.1 copy-start.3
  602.9 0.9 copy-start.5
  603.7 201.5 %all-reduce.24.cloned.1.call-start = ((), (), s32[]{:S(2)}) async-start(), calls=%async_computation.5 | async-start | bytes 1474560
  759.1 84.4 %all-reduce.20.cloned.1.call-start = ((), (), s32[]{:S(2)}) async-start(), calls=%async_computation.3 | async-start | bytes 245760
  771.2 75.5 %copy-start.4 = (bf16[192,640]{1,0:T(8,128)(2,1)S(1)}, bf16[192,640]{1,0:T(8,128)(2,1)}, u32[]{:S(2)}) copy-start(bf16[192,640]{1,0:T(8,128)(2,1)} %param.9) | copy-start | bytes 737284
  806.8 309.7 %all-gather.7.cloned.1.call-start = ((), (), s32[]{:S(2)}) async-start(), calls=%async_computation.1 | async-start | bytes 7987200 | tf_op jit(solution)/shard_map/all_gather | solution.py:21
  846.7 2.5 collective-permute-start
  848.0 3.2 copy-start.2
  1132.5 47.9 %copy-start.1 = (f32[192,2]{0,1:T(2,128)S(1)}, f32[192,2]{0,1:T(2,128)}, u32[]{:S(2)}) copy-start(f32[192,2]{0,1:T(2,128)} %param.10) | copy-start | bytes 4612
  1136.2 43.4 %collective-permute-start.3 = (f32[192,640]{1,0:T(8,128)S(1)}, f32[192,640]{1,0:T(8,128)S(1)}, u32[]{:S(2)}, u32[]{:S(2)}) collective-permute-start(f32[192,640]{1,0:T(8,128)S(1)} %constant_dynamic-slice_fusion.6), channel_id=1, source_target_pairs={{0,64},{64,0},{128,192},{192,128},{1,65},{65,1},{129,193},{193,129... | collective-permute-start | bytes 1474568 | tf_op jit(solution)/shard_map/ppermute | solution.py:16
Sparse Core Ops, SparseCore 0:
  9.1 269.6 all-gather.4
  328.2 133.6 all-reduce.17
  464.6 135.1 all-reduce.25
  603.9 151.6 all-reduce.21
  759.2 45.9 all-reduce.23
  807.6 35.7 all-reduce.19
  846.8 269.7 all-gather.6
where the time goes:
time: 1190 us
  waiting for transfers between devices  1000 us (84%)
  local copies, waits for them, and re-layouts  88.1 us (7%)
  starting transfers between devices  46.8 us (4%)
  other arithmetic  17.5 us (1%)
  between operations  17.4 us (1%)
  matrix products  15 us (1%)
    all_gather x2, waiting for transfers between devices, in_one_piece(): whole, at, done = (lax.all_gather(both, axis, axis=dim, tiled=True), 0, [])  529 us
    unnamed x12, waiting for transfers between devices  470 us
    unnamed x31, local copies, waits for them, and re-layouts  48.6 us
    ppermute x4, starting transfers between devices, swapped(): return lax.ppermute(value, axis, pairs)  46.6 us
  transfers between devices with their start and end apart: 11, of which 10 were waited for; matrix products, arithmetic and copies ran while one was open for 3% of the time, Pallas kernels for 0%

commit v1 on v0

v1 whole, which is shorter than its diff:
```python
import jax
import jax.numpy as jnp
from jax import lax
from jax.experimental import pallas as pl
from jax.experimental.pallas import tpu as pltpu
from jax.sharding import Mesh
from jax.sharding import PartitionSpec as P

EPS = 1e-06
MESH = pl.DeviceIdType.MESH
F32 = jnp.float32
BF16 = jnp.bfloat16

NX, NZ = 4, 8
TOK = 192
DC = 640
U = 384
ROWS = 80
PIECE = 20
PADDED = 32
HALF = TOK // 2
HR = (48, 32, 48)
OPP, LEFT, RIGHT, OWN = 0, 1, 2, 3


def dot(a, b):
    return jnp.dot(a, b, preferred_element_type=F32)


def dot_nt(a, b):
    return lax.dot_general(a, b, (((1,), (1,)), ((), ())), preferred_element_type=F32)


def square_sums(v):
    f = v.astype(F32)
    return jnp.sum(f * f, axis=0, keepdims=True)


def kernel(
    k_ref, v_ref, q_ref, s_ref, w1_ref, w3_ref, w2_ref, out_ref,
    wsend, warr, wg, perm, wcur, kbuf, obuf, qbuf, kt, ot, ps, pr, gg, hid, gbuf,
    rss, rsr, ys, yr, nw, sms, smr, qs, qr, qh, ob, obr, fin, send_sem, recv_sem, loc_sem,
):
    yh = lax.axis_index("yh")
    c = lax.axis_index("core")
    x = lax.axis_index("x")
    y = lax.axis_index("yl")
    z = lax.axis_index("z")
    xr, xl = {"x": lax.rem(x + 1, NX)}, {"x": lax.rem(x + NX - 1, NX)}
    zr, zl = {"z": lax.rem(z + 1, NZ)}, {"z": lax.rem(z + NZ - 1, NZ)}
    peer, ypeer = {"core": 1 - c}, {"yl": 1 - y}
    xhalf = x // 2
    xlow = lax.rem(x, 2)
    own_w = xhalf == c

    def wtarget(j, dy):
        return {"x": 2 * c + j, "core": xhalf, "yl": y if dy == 0 else 1 - y}

    counter = [0]
    sends = []

    def ids(n):
        first = counter[0]
        counter[0] += n
        return first

    def copy(src, dst, k, to):
        return pltpu.make_async_remote_copy(
            src_ref=src, dst_ref=dst, send_sem=send_sem.at[k], recv_sem=recv_sem.at[k],
            device_id=to, device_id_type=MESH,
        )

    def send(src, dst, k, to):
        cp = copy(src, dst, k, to)
        cp.start()
        sends.append(cp)

    def arrived(ref, k, frm):
        copy(ref, ref, k, frm).wait_recv()

    barrier = pltpu.get_barrier_semaphore()
    for to in (peer, xr, xl, zr, zl, ypeer, wtarget(0, 1), wtarget(1, 1)):
        pl.semaphore_signal(barrier, inc=1, device_id=to, device_id_type=MESH)
    for j in range(2):
        @pl.when(jnp.logical_not(jnp.logical_and(own_w, xlow == j)))
        def _():
            pl.semaphore_signal(barrier, inc=1, device_id=wtarget(j, 0), device_id_type=MESH)

    wsend[...] = jnp.zeros_like(wsend)
    for m, w in enumerate((w1_ref, w3_ref, w2_ref)):
        for j in range(2):
            wsend[j, 0:PIECE, m * U:(m + 1) * U] = w[:, j * U:(j + 1) * U]
    pl.semaphore_wait(barrier, 10 - jnp.where(own_w, 1, 0))

    k_w = ids(4)
    slot = 2 * xlow + y
    w_copies = []
    for j in range(2):
        for dy in (1, 0):
            cp = pltpu.make_async_remote_copy(
                src_ref=wsend.at[j], dst_ref=warr.at[slot],
                send_sem=send_sem.at[k_w + 2 * j + dy], recv_sem=recv_sem.at[k_w + slot],
                device_id=wtarget(j, dy), device_id_type=MESH,
            )
            if dy == 1:
                cp.start()
                sends.append(cp)
            else:
                is_self = jnp.logical_and(own_w, xlow == j)
                w_copies.append((is_self, cp))
                lc = pltpu.make_async_copy(wsend.at[j], warr.at[slot], loc_sem.at[j])
                pl.when(jnp.logical_not(is_self))(cp.start)

                @pl.when(is_self)
                def _():
                    lc.start()
                    lc.wait()

    def x_out(src, buf, k):
        send(src, buf.at[LEFT], k, xr)
        send(src, buf.at[RIGHT], k + 1, xl)

    def x_relay(buf, k):
        arrived(buf.at[LEFT], k, xl)
        send(buf.at[LEFT, 0:HALF], buf.at[OPP, 0:HALF], k + 2, xr)
        arrived(buf.at[RIGHT], k + 1, xr)
        send(buf.at[RIGHT, HALF:TOK], buf.at[OPP, HALF:TOK], k + 3, xl)

    def x_last(buf, k):
        arrived(buf.at[OPP, 0:HALF], k + 2, xl)
        arrived(buf.at[OPP, HALF:TOK], k + 3, xr)

    k_k, k_o, k_q = ids(4), ids(4), ids(4)
    x_out(k_ref, kbuf, k_k)
    rates = jnp.where(yh == 0, s_ref[:, 0:1], s_ref[:, 1:2])
    obuf[OWN] = (-(rates * v_ref[...].astype(F32))).astype(BF16)
    x_out(obuf.at[OWN], obuf, k_o)
    kbuf[OWN] = k_ref[...]
    qbuf[OWN] = q_ref[...]

    row = lax.broadcasted_iota(jnp.int32, (DC, DC), 0)
    col = lax.broadcasted_iota(jnp.int32, (DC, DC), 1)
    group = (row >= 160).astype(jnp.int32) + (row >= 320).astype(jnp.int32) + (row >= 480).astype(jnp.int32)
    rem = row - 160 * group
    step20 = jnp.zeros_like(rem)
    for t in range(1, NZ):
        step20 = step20 + (rem >= PIECE * t).astype(jnp.int32)
    wanted = ROWS * step20 + PIECE * group + rem - PIECE * step20
    perm[...] = jnp.where(col == wanted, 1.0, 0.0).astype(BF16)

    for s in range(4):
        from_x, from_y = s // 2, s % 2
        here = jnp.logical_and(jnp.logical_and(own_w, xlow == from_x), y == from_y)

        @pl.when(jnp.logical_not(here))
        def _():
            copy(warr.at[s], warr.at[s], k_w + s, ypeer).wait_recv()

    prow = lax.broadcasted_iota(jnp.int32, (ROWS, 4 * PADDED), 0)
    pcol = lax.broadcasted_iota(jnp.int32, (ROWS, 4 * PADDED), 1)
    pgroup = (prow >= 20).astype(jnp.int32) + (prow >= 40).astype(jnp.int32) + (prow >= 60).astype(jnp.int32)
    pack = jnp.where(pcol == prow + (PADDED - PIECE) * pgroup, 1.0, 0.0).astype(BF16)
    packed = dot(pack, warr[...].reshape(4 * PADDED, 3 * U)).astype(BF16)
    for m in range(3):
        wg[z, m] = packed[:, m * U:(m + 1) * U]

    def part(buf, at, m, step, way):
        if step < 4:
            return buf.at[at, m]
        lo, hi = (0, HR[m]) if way == 0 else (HR[m], ROWS)
        return buf.at[at, m, lo:hi]

    def zpos(off):
        return lax.rem(z + off + 2 * NZ, NZ)

    def ring_send(buf, k, step, m):
        for way, (sign, to) in enumerate(((-1, zr), (1, zl))):
            ref = part(buf, zpos(sign * (step - 1)), m, step, way)
            send(ref, ref, k + (step - 1) * 6 + 2 * m + way, to)

    def ring_arrived(buf, k, step, m):
        for way, (sign, frm) in enumerate(((-1, zl), (1, zr))):
            ref = part(buf, zpos(sign * step), m, step, way)
            arrived(ref, k + (step - 1) * 6 + 2 * m + way, frm)

    k_g = ids(24)
    for m in range(3):
        ring_send(wg, k_g, 1, m)
    for step in range(2, 5):
        for m in range(3):
            ring_arrived(wg, k_g, step - 1, m)
            ring_send(wg, k_g, step, m)
        if step == 2:
            x_relay(kbuf, k_k)
        if step == 3:
            x_relay(obuf, k_o)
            x_out(q_ref, qbuf, k_q)
            x_last(kbuf, k_k)
            for h in range(2):
                kt[:, h * U:(h + 1) * U] = kbuf[2 * h:2 * h + 2].reshape(2 * TOK, DC).T
    for m in range(3):
        ring_arrived(wg, k_g, 4, m)
    for m in range(3):
        wcur[:, m * U:(m + 1) * U] = dot(perm[...], wg[:, m].reshape(DC, U)).astype(BF16)
    x_last(obuf, k_o)

    k_p = ids(4)

    def p_copy(b):
        return copy(ps.at[b], pr.at[b], k_p + b, peer)

    @pl.loop(0, 4)
    def _(b):
        ps[b, :, 0:2 * U] = dot(kbuf[b], wcur[:, 0:2 * U])
        ps[b, :, 2 * U:3 * U] = dot(obuf[b], wcur[:, 2 * U:3 * U])
        p_copy(b).start()

    for h in range(2):
        ot[:, h * U:(h + 1) * U] = obuf[2 * h:2 * h + 2].reshape(2 * TOK, DC).T

    @pl.loop(0, 4)
    def _(b):
        p_copy(b).wait_recv()

        @pl.loop(0, TOK // 16)
        def _(t):
            r = pl.ds(pl.multiple_of(t * 16, 16), 16)
            o = pl.ds(pl.multiple_of(b * TOK + t * 16, 16), 16)
            gate = ps[b, r, 0:U] + pr[b, r, 0:U]
            up = ps[b, r, U:2 * U] + pr[b, r, U:2 * U]
            hg = ps[b, r, 2 * U:3 * U] + pr[b, r, 2 * U:3 * U]
            sg = jax.nn.sigmoid(gate)
            silu = gate * sg
            hid[o, :] = (silu * up).astype(BF16)
            gg[o, 0:U] = (hg * up * (sg * (1.0 + gate * (1.0 - sg)))).astype(BF16)
            gg[o, U:2 * U] = (hg * silu).astype(BF16)

    k_r = ids(24)

    def rs_id(step, m, way):
        return k_r + (step - 1) * 6 + 2 * m + way

    far = pl.ds(pl.multiple_of(zpos(4) * ROWS, 16), ROWS)
    g13 = dot(kt[far, :], gg[...])
    g2 = dot(ot[far, :], hid[...])
    for m, g in enumerate((g13[:, 0:U], g13[:, U:2 * U], g2)):
        rss[0, 0, m] = g.astype(BF16)
        for way, to in enumerate((zr, zl)):
            lo, hi = (0, HR[m]) if way == 0 else (HR[m], ROWS)
            send(rss.at[0, 0, m, lo:hi], rsr.at[way, 0, m, lo:hi], rs_id(1, m, way), to)
    for m in range(3):
        g = dot(kt[...], gg[:, m * U:(m + 1) * U]) if m < 2 else dot(ot[...], hid[...])
        gbuf[:, m] = g.reshape(NZ, ROWS, U)

    for step in range(2, 5):
        for m in range(3):
            for way, (sign, to, frm) in enumerate(((1, zr, zl), (-1, zl, zr))):
                at = zpos(sign * (5 - step))
                if step == 2:
                    lo, hi = (0, HR[m]) if way == 0 else (HR[m], ROWS)
                    olo, ohi = (HR[m], ROWS) if way == 0 else (0, HR[m])
                    arrived(rsr.at[way, 0, m, lo:hi], rs_id(1, m, way), frm)
                    rss[way, 1, m, lo:hi] = (gbuf[at, m, lo:hi] + rsr[way, 0, m, lo:hi].astype(F32)).astype(BF16)
                    rss[way, 1, m, olo:ohi] = gbuf[at, m, olo:ohi].astype(BF16)
                else:
                    arrived(rsr.at[way, step - 2, m], rs_id(step - 1, m, way), frm)
                    rss[way, step - 1, m] = (gbuf[at, m] + rsr[way, step - 2, m].astype(F32)).astype(BF16)
                send(rss.at[way, step - 1, m], rsr.at[way, step - 1, m], rs_id(step, m, way), to)
        if step == 2:
            old = [square_sums(wcur[:, m * U:(m + 1) * U]) for m in range(3)]
            for m in range(3):
                sms[m:m + 1, :] = old[m]
        if step == 3:
            x_relay(qbuf, k_q)

    k_y = ids(3)
    for m in range(3):
        for way, frm in enumerate((zl, zr)):
            arrived(rsr.at[way, 3, m], rs_id(4, m, way), frm)
        total = gbuf[z, m] + rsr[0, 3, m].astype(F32) + rsr[1, 3, m].astype(F32)
        gbuf[z, m] = total
        ys[m] = total.astype(BF16)
        send(ys.at[m], yr.at[m], k_y + m, ypeer)
    x_last(qbuf, k_q)
    own_rows = pl.ds(pl.multiple_of(z * ROWS, 16), ROWS)
    k_n = ids(24)
    new_sums = []
    for m in range(3):
        arrived(yr.at[m], k_y + m, ypeer)
        old_w = wcur[own_rows, m * U:(m + 1) * U].astype(F32)
        nw[z, m] = (old_w - (gbuf[z, m] + yr[m].astype(F32))).astype(BF16)
        ring_send(nw, k_n, 1, m)
        new_sums.append(square_sums(nw[z, m]))
    for step in range(2, 6):
        for m in range(3):
            ring_arrived(nw, k_n, step - 1, m)
            if step < 5:
                ring_send(nw, k_n, step, m)
                for sign in (-1, 1):
                    new_sums[m] = new_sums[m] + square_sums(nw[zpos(sign * (step - 1)), m])
            else:
                new_sums[m] = new_sums[m] + square_sums(nw[zpos(4), m])
    for m in range(3):
        sms[3 + m:4 + m, :] = new_sums[m]
    sms[6:8, :] = jnp.zeros((2, U), F32)
    k_s = ids(1)
    send(sms, smr, k_s, peer)

    k_qp = ids(4)

    def q_copy(b):
        return copy(qs.at[b], qr.at[b], k_qp + b, peer)

    @pl.loop(0, 4)
    def _(b):
        for m in range(2):
            qs[b, :, m * U:(m + 1) * U] = dot(qbuf[b], nw[:, m].reshape(DC, U))
        q_copy(b).start()

    arrived(smr, k_s, peer)
    sums = sms[...] + smr[...]
    r1, r3, r2 = [jnp.sqrt((sums[m:m + 1] + EPS) / (sums[3 + m:4 + m] + EPS)) for m in range(3)]

    k_x = ids(4)
    for b in range(4):
        q_copy(b).wait_recv()

        @pl.loop(0, TOK // 16)
        def _(t):
            r = pl.ds(pl.multiple_of(t * 16, 16), 16)
            qg = (qs[b, r, 0:U] + qr[b, r, 0:U]) * r1
            qu = (qs[b, r, U:2 * U] + qr[b, r, U:2 * U]) * r3
            qh[b, r, :] = (qg * jax.nn.sigmoid(qg) * qu * r2).astype(BF16)

        part_out = dot_nt(qh[b], nw[:, 2].reshape(DC, U))
        if b == OPP:
            ob[OPP] = part_out.astype(BF16)
            send(ob.at[OPP, 0:HALF], obr.at[0:HALF], k_x, xr)
            send(ob.at[OPP, HALF:TOK], obr.at[HALF:TOK], k_x + 1, xl)
        elif b == LEFT:
            ob[LEFT, 0:HALF] = part_out[0:HALF].astype(BF16)
            arrived(obr.at[HALF:TOK], k_x + 1, xr)
            ob[LEFT, HALF:TOK] = (part_out[HALF:TOK] + obr[HALF:TOK].astype(F32)).astype(BF16)
            send(ob.at[LEFT], fin.at[1], k_x + 2, xl)
        elif b == RIGHT:
            ob[RIGHT, HALF:TOK] = part_out[HALF:TOK].astype(BF16)
            arrived(obr.at[0:HALF], k_x, xl)
            ob[RIGHT, 0:HALF] = (part_out[0:HALF] + obr[0:HALF].astype(F32)).astype(BF16)
            send(ob.at[RIGHT], fin.at[0], k_x + 3, xr)
        else:
            arrived(fin.at[1], k_x + 2, xr)
            arrived(fin.at[0], k_x + 3, xl)
            out_ref[...] = (part_out + fin[0].astype(F32) + fin[1].astype(F32)).astype(BF16)

    for cp in sends:
        cp.wait_send()
    for is_self, cp in w_copies:
        pl.when(jnp.logical_not(is_self))(cp.wait_send)

    @pl.loop(0, 4)
    def _(b):
        p_copy(b).wait_send()
        q_copy(b).wait_send()


N_SEM = 4 + 12 + 24 + 4 + 24 + 3 + 24 + 1 + 4 + 4


def body(keys, values, queries, step_size, gate_weight, up_weight, down_weight):
    vmem = pl.BlockSpec(memory_space=pltpu.VMEM)
    return pl.pallas_call(
        kernel,
        out_shape=jax.ShapeDtypeStruct((TOK, DC), BF16),
        in_specs=[vmem] * 7,
        out_specs=vmem,
        scratch_shapes=[
            pltpu.VMEM((2, PADDED, 3 * U), BF16),
            pltpu.VMEM((4, PADDED, 3 * U), BF16),
            pltpu.VMEM((NZ, 3, ROWS, U), BF16),
            pltpu.VMEM((DC, DC), BF16),
            pltpu.VMEM((DC, 3 * U), BF16),
            pltpu.VMEM((4, TOK, DC), BF16),
            pltpu.VMEM((4, TOK, DC), BF16),
            pltpu.VMEM((4, TOK, DC), BF16),
            pltpu.VMEM((DC, 4 * TOK), BF16),
            pltpu.VMEM((DC, 4 * TOK), BF16),
            pltpu.VMEM((4, TOK, 3 * U), F32),
            pltpu.VMEM((4, TOK, 3 * U), F32),
            pltpu.VMEM((4 * TOK, 2 * U), BF16),
            pltpu.VMEM((4 * TOK, U), BF16),
            pltpu.VMEM((NZ, 3, ROWS, U), F32),
            pltpu.VMEM((2, 4, 3, ROWS, U), BF16),
            pltpu.VMEM((2, 4, 3, ROWS, U), BF16),
            pltpu.VMEM((3, ROWS, U), BF16),
            pltpu.VMEM((3, ROWS, U), BF16),
            pltpu.VMEM((NZ, 3, ROWS, U), BF16),
            pltpu.VMEM((8, U), F32),
            pltpu.VMEM((8, U), F32),
            pltpu.VMEM((4, TOK, 2 * U), F32),
            pltpu.VMEM((4, TOK, 2 * U), F32),
            pltpu.VMEM((4, TOK, U), BF16),
            pltpu.VMEM((4, TOK, DC), BF16),
            pltpu.VMEM((TOK, DC), BF16),
            pltpu.VMEM((2, TOK, DC), BF16),
            pltpu.SemaphoreType.DMA((N_SEM,)),
            pltpu.SemaphoreType.DMA((N_SEM,)),
            pltpu.SemaphoreType.DMA((2,)),
        ],
        compiler_params=pltpu.CompilerParams(
            collective_id=0, has_side_effects=True, vmem_limit_bytes=60 << 20
        ),
        name="ttt_layer",
    )(keys, values, queries, step_size, gate_weight, up_weight, down_weight)


def solution(mesh):
    finer = Mesh(mesh.devices.reshape(2, 2, 4, 2, 8), ("yh", "core", "x", "yl", "z"))
    seq, head = ("x", "yl", "z"), ("yh", "core")
    placed = (
        P(seq, head), P(seq, head), P(seq, head), P(seq, None),
        P(seq, head), P(seq, head), P(seq, head),
    )
    return jax.shard_map(body, mesh=finer, in_specs=placed, out_specs=P(seq, head), check_vma=False)
```

time: 1190 us -> 102 us (0.09)
  waiting for transfers between devices: 1000 us -> 0 us
  Pallas kernels: 0 us -> 98.7 us
  local copies, waits for them, and re-layouts: 88.1 us -> 3.1 us
  starting transfers between devices: 46.8 us -> 0 us
  other arithmetic: 17.5 us -> 0 us
  between operations: 17.4 us -> 0.01 us
  matrix products: 15 us -> 0 us
    all_gather x2 -> x0, waiting for transfers between devices: 529 us -> none  [in_one_piece(): whole, at, done = (lax.all_gather(both, axis, axis=dim, tiled=True), 0, [])]
    unnamed x12 -> x0, waiting for transfers between devices: 470 us -> none
    pallas_call x0 -> x1, Pallas kernels: none -> 98.7 us  [body(): pl.pallas_call(kernel, out_shape=jax.ShapeDtypeStruct((TOK, DC), BF16), i...]
    ppermute x4 -> x0, starting transfers between devices: 46.6 us -> none  [swapped(): return lax.ppermute(value, axis, pairs)]
    unnamed x31 -> x2, local copies, waits for them, and re-layouts: 48.6 us -> 3.1 us
    dot_general x8 -> x0, matrix products: 15 us -> none  [the longest x1 3.68 us: body(): jnp.dot(query_hidden, pieces[2], preferred_element_type=jnp.float32)]
    reshape x1 -> x0, local copies, waits for them, and re-layouts: 13.3 us -> none  [split_up(): return jnp.moveaxis(value.reshape(*before, peers, -1, *after), dim, 0)]
    split x1 -> x0, local copies, waits for them, and re-layouts: 12.7 us -> none  [spread_scatter(): jnp.split(pieces, cut_rows(pieces.shape[split_at], count), axis=split_at)]
  transfers between devices with their start and end apart: 11 -> 0, of which waited for: 10 -> 0; matrix products, arithmetic and copies ran while one was open for 3% -> 0% of each run, Pallas kernels for 0% -> 0%
where the time goes in v1:
time: 102 us
  Pallas kernels  98.7 us (97%)
  local copies, waits for them, and re-layouts  3.1 us (3%)
    pallas_call x1, Pallas kernels, body(): pl.pallas_call(kernel, out_shape=jax.ShapeDtypeStruct((TOK, DC), BF16), i...  98.7 us
    unnamed x2, local copies, waits for them, and re-layouts  3.1 us

profile of v1, /device:TPU:1, one launch (start us, length us, event | category | flops | bytes accessed | tf_op | source)
XLA Modules:
  0.0 101.8 jit_solution(5776256650284195891)
XLA Ops:
  0.0 1.4 %copy.8.s_ref = f32[192,2]{1,0:T(8,128)} copy(f32[192,2]{0,1:T(2,128)} %param.10) | data formatting | bytes 3072 | tf_op args[3]
  1.4 98.7 %ttt_layer.1 = bf16[192,640]{1,0:T(8,128)(2,1)} custom-call(bf16[192,640]{1,0:T(8,128)(2,1)} %k_ref.1, bf16[192,640]{1,0:T(8,128)(2,1)} %v_ref.1, bf16[192,640]{1,0:T(8,128)(2,1)} %q_ref.1, f32[192,2]{1,0:T(8,128)} %copy.8.s_ref, bf16[20,768]{1,0:T(8,128)(2,1)} %w1_ref.1, bf16[20,768]{1,0:T(8,128)(2,1)} %w3_ref.1, bf16[20,768]{1,0:T(8,128)(2,1)} %w2_ref.1), custom_call_target="tpu_custom_call" | custom-call | tf_op jit(solution)/shard_map/ttt_layer/pallas_call | solution.py:371
  100.1 1.7 %copy.10 = bf16[192,640]{1,0:T(8,128)(2,1)} copy(bf16[192,640]{1,0:T(8,128)(2,1)} %ttt_layer.1) | data formatting | bytes 491520

commit v2 on v1

v2 whole, which is shorter than its diff:
```python
import jax
import jax.numpy as jnp
from jax import lax
from jax.experimental import pallas as pl
from jax.experimental.pallas import tpu as pltpu
from jax.sharding import Mesh
from jax.sharding import PartitionSpec as P

EPS = 1e-06
MESH = pl.DeviceIdType.MESH
F32 = jnp.float32
BF16 = jnp.bfloat16

NX, NZ = 4, 8
TOK = 192
DC = 640
U = 384
ROWS = 80
PIECE = 20
PADDED = 32
HALF = TOK // 2
CUT = ((0, 48), (48, ROWS))
CHUNKS = ((0, 0), (0, 1), (1, 0), (1, 1))
OPP, LEFT, RIGHT, OWN = 0, 1, 2, 3
STEP = 32


def dot(a, b):
    return jnp.dot(a, b, preferred_element_type=F32)


def dot_nt(a, b):
    return lax.dot_general(a, b, (((1,), (1,)), ((), ())), preferred_element_type=F32)


def square_sums(v):
    f = v.astype(F32)
    return jnp.sum(f * f, axis=0, keepdims=True)


def far_way(kind, h):
    return h if kind == 0 else 1 - h


def kernel(
    k_hbm, v_hbm, q_hbm, s_hbm, w1_hbm, w3_hbm, w2_hbm, out_ref,
    win, vin, sin, wsend, warr, wg, perm, wcur, kbuf, obuf, qbuf, kt, ot, ps, pr, gg, hid,
    ga, gb, ysf, ysend, yrecv, rss, rsr, ybs, ybr, nw, sms, smr, qs, qr, qh, ob, op, obr, fin,
    send_sem, recv_sem, loc_sem,
):
    yh = lax.axis_index("yh")
    c = lax.axis_index("core")
    x = lax.axis_index("x")
    y = lax.axis_index("yl")
    z = lax.axis_index("z")
    xr, xl = {"x": lax.rem(x + 1, NX)}, {"x": lax.rem(x + NX - 1, NX)}
    zr, zl = {"z": lax.rem(z + 1, NZ)}, {"z": lax.rem(z + NZ - 1, NZ)}
    peer, ypeer = {"core": 1 - c}, {"yl": 1 - y}
    xhalf = x // 2
    xlow = lax.rem(x, 2)
    own_w = xhalf == c

    def wtarget(j, dy):
        return {"x": 2 * c + j, "core": xhalf, "yl": y if dy == 0 else 1 - y}

    counter = [0]
    sends = []

    def ids(n):
        first = counter[0]
        counter[0] += n
        return first

    def copy(src, dst, k, to):
        return pltpu.make_async_remote_copy(
            src_ref=src, dst_ref=dst, send_sem=send_sem.at[k], recv_sem=recv_sem.at[k],
            device_id=to, device_id_type=MESH,
        )

    def send(src, dst, k, to):
        cp = copy(src, dst, k, to)
        cp.start()
        sends.append(cp)

    def arrived(ref, k, frm):
        copy(ref, ref, k, frm).wait_recv()

    barrier = pltpu.get_barrier_semaphore()
    for to in (peer, xr, xl, zr, zl, ypeer, wtarget(0, 1), wtarget(1, 1)):
        pl.semaphore_signal(barrier, inc=1, device_id=to, device_id_type=MESH)
    for j in range(2):
        @pl.when(jnp.logical_not(jnp.logical_and(own_w, xlow == j)))
        def _():
            pl.semaphore_signal(barrier, inc=1, device_id=wtarget(j, 0), device_id_type=MESH)

    loads = [
        pltpu.make_async_copy(w1_hbm, win.at[0], loc_sem.at[0]),
        pltpu.make_async_copy(w3_hbm, win.at[1], loc_sem.at[1]),
        pltpu.make_async_copy(w2_hbm, win.at[2], loc_sem.at[2]),
        pltpu.make_async_copy(k_hbm, kbuf.at[OWN], loc_sem.at[3]),
        pltpu.make_async_copy(v_hbm, vin, loc_sem.at[4]),
        pltpu.make_async_copy(s_hbm, sin, loc_sem.at[5]),
        pltpu.make_async_copy(q_hbm, qbuf.at[OWN], loc_sem.at[6]),
    ]
    for ld in loads:
        ld.start()

    wsend[...] = jnp.zeros_like(wsend)
    for m in range(3):
        loads[m].wait()
    for j in range(2):
        for t in range(2):
            wsend[j, t, 0:PIECE, 0:U] = win[t, :, j * U:(j + 1) * U]
            wsend[j, t, 0:PIECE, U:2 * U] = win[2, :, j * U:(j + 1) * U]
    loads[3].wait()
    pl.semaphore_wait(barrier, 10 - jnp.where(own_w, 1, 0))

    k_w = ids(4)
    slot = 2 * xlow + y
    w_copies = []
    for j in range(2):
        for dy in (1, 0):
            block = wsend.at[j, y if dy == 0 else 1 - y]
            cp = pltpu.make_async_remote_copy(
                src_ref=block, dst_ref=warr.at[slot],
                send_sem=send_sem.at[k_w + 2 * j + dy], recv_sem=recv_sem.at[k_w + slot],
                device_id=wtarget(j, dy), device_id_type=MESH,
            )
            if dy == 1:
                cp.start()
                sends.append(cp)
            else:
                is_self = jnp.logical_and(own_w, xlow == j)
                w_copies.append((is_self, cp))
                lc = pltpu.make_async_copy(block, warr.at[slot], loc_sem.at[7 + j])
                pl.when(jnp.logical_not(is_self))(cp.start)

                @pl.when(is_self)
                def _():
                    lc.start()
                    lc.wait()

    def x_out(buf, k):
        send(buf.at[OWN], buf.at[LEFT], k, xr)
        send(buf.at[OWN], buf.at[RIGHT], k + 1, xl)

    def x_relay(buf, k):
        arrived(buf.at[LEFT], k, xl)
        send(buf.at[LEFT, 0:HALF], buf.at[OPP, 0:HALF], k + 2, xr)
        arrived(buf.at[RIGHT], k + 1, xr)
        send(buf.at[RIGHT, HALF:TOK], buf.at[OPP, HALF:TOK], k + 3, xl)

    def x_last(buf, k):
        arrived(buf.at[OPP, 0:HALF], k + 2, xl)
        arrived(buf.at[OPP, HALF:TOK], k + 3, xr)

    k_k, k_o, k_q = ids(4), ids(4), ids(4)
    x_out(kbuf, k_k)
    loads[4].wait()
    loads[5].wait()
    diag = lax.broadcasted_iota(jnp.int32, (TOK, TOK), 0) == lax.broadcasted_iota(jnp.int32, (TOK, TOK), 1)
    rate_row = jnp.where(yh == 0, sin[0:1, :], sin[1:2, :])
    rates = jnp.sum(jnp.where(diag, rate_row, 0.0), axis=1, keepdims=True)
    obuf[OWN] = (-(rates * vin[...].astype(F32))).astype(BF16)
    x_out(obuf, k_o)

    row = lax.broadcasted_iota(jnp.int32, (DC, DC), 0)
    col = lax.broadcasted_iota(jnp.int32, (DC, DC), 1)
    group = (row >= 160).astype(jnp.int32) + (row >= 320).astype(jnp.int32) + (row >= 480).astype(jnp.int32)
    rem = row - 160 * group
    step20 = jnp.zeros_like(rem)
    for t in range(1, NZ):
        step20 = step20 + (rem >= PIECE * t).astype(jnp.int32)
    wanted = ROWS * step20 + PIECE * group + rem - PIECE * step20
    perm[...] = jnp.where(col == wanted, 1.0, 0.0).astype(BF16)

    for s in range(4):
        from_x, from_y = s // 2, s % 2
        here = jnp.logical_and(jnp.logical_and(own_w, xlow == from_x), y == from_y)

        @pl.when(jnp.logical_not(here))
        def _():
            copy(warr.at[s], warr.at[s], k_w + s, ypeer).wait_recv()

    prow = lax.broadcasted_iota(jnp.int32, (ROWS, 4 * PADDED), 0)
    pcol = lax.broadcasted_iota(jnp.int32, (ROWS, 4 * PADDED), 1)
    pgroup = (prow >= 20).astype(jnp.int32) + (prow >= 40).astype(jnp.int32) + (prow >= 60).astype(jnp.int32)
    pack = jnp.where(pcol == prow + (PADDED - PIECE) * pgroup, 1.0, 0.0).astype(BF16)
    packed = dot(pack, warr[...].reshape(4 * PADDED, 2 * U)).astype(BF16)
    wg[z, y] = packed[:, 0:U]
    wg[z, 2] = packed[:, U:2 * U]

    def zpos(off):
        return lax.rem(z + off + 2 * NZ, NZ)

    def chunk(buf, at, kind, h):
        return buf.at[at, y if kind == 0 else 2, CUT[h][0]:CUT[h][1]]

    def ways(step, kind, h):
        return (0, 1) if step < 4 else (far_way(kind, h),)

    def ring_id(k, step, kind, h, way):
        return k + (step - 1) * 8 + 4 * kind + 2 * h + way

    def ring_send(buf, k, step, kind, h):
        for way in ways(step, kind, h):
            ref = chunk(buf, zpos((1 - step) if way == 0 else (step - 1)), kind, h)
            send(ref, ref, ring_id(k, step, kind, h, way), zr if way == 0 else zl)

    def ring_arrived(buf, k, step, kind, h):
        for way in ways(step, kind, h):
            ref = chunk(buf, zpos(-step if way == 0 else step), kind, h)
            arrived(ref, ring_id(k, step, kind, h, way), zl if way == 0 else zr)

    def offsets(step):
        return ((0,), (-1, 1), (-2, 2), (-3, 3), (4,))[step]

    def pair_send(buf, k, step):
        for i, off in enumerate(offsets(step)):
            at = zpos(off)
            send(buf.at[at, y], buf.at[at, y], k + 2 * step + i, ypeer)

    def pair_arrived(buf, k, step):
        for i, off in enumerate(offsets(step)):
            arrived(buf.at[zpos(off), 1 - y], k + 2 * step + i, ypeer)

    def gather(buf, k, k_pair, step):
        for kind, h in CHUNKS:
            if step > 1:
                ring_arrived(buf, k, step - 1, kind, h)
            ring_send(buf, k, step, kind, h)
            if (kind, h) == (0, 1):
                pair_send(buf, k_pair, step - 1)

    k_g, k_gp = ids(32), ids(10)
    gather(wg, k_g, k_gp, 1)
    gather(wg, k_g, k_gp, 2)
    x_relay(kbuf, k_k)
    gather(wg, k_g, k_gp, 3)
    gather(wg, k_g, k_gp, 4)
    x_relay(obuf, k_o)
    loads[6].wait()
    x_out(qbuf, k_q)
    for h in range(2):
        ring_arrived(wg, k_g, 4, 0, h)
    pair_send(wg, k_gp, 4)
    for h in range(2):
        ring_arrived(wg, k_g, 4, 1, h)
    x_last(kbuf, k_k)
    for h in range(2):
        kt[:, h * U:(h + 1) * U] = kbuf[2 * h:2 * h + 2].reshape(2 * TOK, DC).T
    wcur[:, 2 * U:3 * U] = dot(perm[...], wg[:, 2].reshape(DC, U)).astype(BF16)
    for step in range(5):
        pair_arrived(wg, k_gp, step)
    for m in range(2):
        wcur[:, m * U:(m + 1) * U] = dot(perm[...], wg[:, m].reshape(DC, U)).astype(BF16)

    k_p = ids(4)

    def p_copy(b):
        return copy(ps.at[b], pr.at[b], k_p + b, peer)

    @pl.loop(0, 4)
    def _(i):
        b = 3 - i
        pl.when(i == 3)(lambda: x_last(obuf, k_o))
        ps[b, :, 0:2 * U] = dot(kbuf[b], wcur[:, 0:2 * U])
        ps[b, :, 2 * U:3 * U] = dot(obuf[b], wcur[:, 2 * U:3 * U])
        p_copy(b).start()

    for h in range(2):
        ot[:, h * U:(h + 1) * U] = obuf[2 * h:2 * h + 2].reshape(2 * TOK, DC).T

    @pl.loop(0, 4)
    def _(i):
        b = 3 - i
        p_copy(b).wait_recv()

        @pl.loop(0, TOK // STEP)
        def _(t):
            r = pl.ds(pl.multiple_of(t * STEP, STEP), STEP)
            o = pl.ds(pl.multiple_of(b * TOK + t * STEP, STEP), STEP)
            gate = ps[b, r, 0:U] + pr[b, r, 0:U]
            up = ps[b, r, U:2 * U] + pr[b, r, U:2 * U]
            hg = ps[b, r, 2 * U:3 * U] + pr[b, r, 2 * U:3 * U]
            sg = jax.nn.sigmoid(gate)
            silu = gate * sg
            hid[o, :] = (silu * up).astype(BF16)
            gg[0, o, :] = (hg * up * (sg * (1.0 + gate * (1.0 - sg)))).astype(BF16)
            gg[1, o, :] = (hg * silu).astype(BF16)

    k_ya = ids(10)
    k_r = ids(32)
    far = pl.ds(pl.multiple_of(zpos(4) * ROWS, 16), ROWS)
    ysf[...] = dot(kt[far, :], gg[1 - y]).astype(BF16)
    send(ysf, yrecv.at[zpos(4)], k_ya + 8, ypeer)
    ysend[...] = dot(kt[...], gg[1 - y]).astype(BF16).reshape(NZ, ROWS, U)
    for step in (3, 2, 1, 0):
        for i, off in enumerate(offsets(step)):
            at = zpos(off)
            send(ysend.at[at], yrecv.at[at], k_ya + 2 * step + i, ypeer)
    gb[...] = dot(ot[...], hid[...]).reshape(NZ, ROWS, U)

    def rs_send(step, kind, h, way):
        lo, hi = CUT[h]
        at = zpos((5 - step) if way == 0 else (step - 5))
        v = (ga if kind == 0 else gb)[at, lo:hi]
        if kind == 0:
            v = v + yrecv[at, lo:hi].astype(F32)
        if step > 2 or (step == 2 and far_way(kind, h) == way):
            arrived(rsr.at[way, step - 2, kind, lo:hi], ring_id(k_r, step - 1, kind, h, way), zl if way == 0 else zr)
            v = v + rsr[way, step - 2, kind, lo:hi].astype(F32)
        rss[way, step - 1, kind, lo:hi] = v.astype(BF16)
        send(
            rss.at[way, step - 1, kind, lo:hi], rsr.at[way, step - 1, kind, lo:hi],
            ring_id(k_r, step, kind, h, way), zr if way == 0 else zl,
        )

    for h in range(2):
        rs_send(1, 1, h, far_way(1, h))
    ga[...] = dot(kt[...], gg[y]).reshape(NZ, ROWS, U)
    arrived(yrecv.at[zpos(4)], k_ya + 8, ypeer)
    for h in range(2):
        rs_send(1, 0, h, far_way(0, h))

    for step in range(2, 5):
        for way in range(2):
            for h in range(2):
                rs_send(step, 1, h, way)
        for way, off in enumerate((5 - step, step - 5)):
            arrived(yrecv.at[zpos(off)], k_ya + 2 * (5 - step) + (1 - way), ypeer)
            for h in range(2):
                rs_send(step, 0, h, way)
        if step == 2:
            for m in range(3):
                sms[m:m + 1, :] = square_sums(wcur[:, m * U:(m + 1) * U])
        if step == 3:
            x_relay(qbuf, k_q)

    def total(kind):
        for way in range(2):
            for h in range(2):
                lo, hi = CUT[h]
                arrived(rsr.at[way, 3, kind, lo:hi], ring_id(k_r, 4, kind, h, way), zl if way == 0 else zr)
        return (ga if kind == 0 else gb)[z] + rsr[0, 3, kind].astype(F32) + rsr[1, 3, kind].astype(F32)

    k_yb = ids(1)
    tb = total(1)
    gb[z] = tb
    ybs[...] = tb.astype(BF16)
    send(ybs, ybr, k_yb, ypeer)
    own_rows = pl.ds(pl.multiple_of(z * ROWS, 16), ROWS)
    arrived(yrecv.at[z], k_ya, ypeer)
    ta = total(0) + yrecv[z].astype(F32)
    old_a = jnp.where(y == 0, wcur[own_rows, 0:U].astype(F32), wcur[own_rows, U:2 * U].astype(F32))
    nw[z, y] = (old_a - ta).astype(BF16)
    k_n, k_np = ids(32), ids(10)
    for h in range(2):
        ring_send(nw, k_n, 1, 0, h)
    pair_send(nw, k_np, 0)
    arrived(ybr, k_yb, ypeer)
    nw[z, 2] = (wcur[own_rows, 2 * U:3 * U].astype(F32) - (gb[z] + ybr[...].astype(F32))).astype(BF16)
    for h in range(2):
        ring_send(nw, k_n, 1, 1, h)
    x_last(qbuf, k_q)
    for step in range(2, 5):
        gather(nw, k_n, k_np, step)
    for h in range(2):
        ring_arrived(nw, k_n, 4, 0, h)
    pair_send(nw, k_np, 4)
    for h in range(2):
        ring_arrived(nw, k_n, 4, 1, h)
    sms[5:6, :] = square_sums(nw[:, 2].reshape(DC, U))
    for step in range(5):
        pair_arrived(nw, k_np, step)

    k_qp = ids(4)
    k_s = ids(1)

    def q_copy(b):
        return copy(qs.at[b], qr.at[b], k_qp + b, peer)

    def q_part(b):
        for m in range(2):
            qs[b, :, m * U:(m + 1) * U] = dot(qbuf[b], nw[:, m].reshape(DC, U))
        cp = q_copy(b)
        cp.start()
        sends.append(cp)

    q_part(OPP)
    for m in range(2):
        sms[3 + m:4 + m, :] = square_sums(nw[:, m].reshape(DC, U))
    sms[6:8, :] = jnp.zeros((2, U), F32)
    send(sms, smr, k_s, peer)
    q_part(LEFT)
    arrived(smr, k_s, peer)
    sums = sms[...] + smr[...]
    r1, r3, r2 = [jnp.sqrt((sums[m:m + 1] + EPS) / (sums[3 + m:4 + m] + EPS)) for m in range(3)]

    def out_part(b):
        q_copy(b).wait_recv()

        @pl.loop(0, TOK // STEP)
        def _(t):
            r = pl.ds(pl.multiple_of(t * STEP, STEP), STEP)
            qg = (qs[b, r, 0:U] + qr[b, r, 0:U]) * r1
            qu = (qs[b, r, U:2 * U] + qr[b, r, U:2 * U]) * r3
            qh[b, r, :] = (qg * jax.nn.sigmoid(qg) * qu * r2).astype(BF16)

        return dot_nt(qh[b], nw[:, 2].reshape(DC, U))

    k_x = ids(6)
    part = out_part(OPP)
    ob[OPP] = part.astype(BF16)
    send(ob.at[OPP, 0:HALF], obr.at[0:HALF], k_x, xr)
    send(ob.at[OPP, HALF:TOK], obr.at[HALF:TOK], k_x + 1, xl)
    q_part(RIGHT)
    part = out_part(LEFT)
    ob[LEFT, 0:HALF] = part[0:HALF].astype(BF16)
    send(ob.at[LEFT, 0:HALF], fin.at[1, 0:HALF], k_x + 2, xl)
    op[0] = part[HALF:TOK]
    q_part(OWN)
    part = out_part(RIGHT)
    ob[RIGHT, HALF:TOK] = part[HALF:TOK].astype(BF16)
    send(ob.at[RIGHT, HALF:TOK], fin.at[0, HALF:TOK], k_x + 4, xr)
    op[1] = part[0:HALF]
    arrived(obr.at[HALF:TOK], k_x + 1, xr)
    ob[LEFT, HALF:TOK] = (op[0] + obr[HALF:TOK].astype(F32)).astype(BF16)
    send(ob.at[LEFT, HALF:TOK], fin.at[1, HALF:TOK], k_x + 3, xl)
    arrived(obr.at[0:HALF], k_x, xl)
    ob[RIGHT, 0:HALF] = (op[1] + obr[0:HALF].astype(F32)).astype(BF16)
    send(ob.at[RIGHT, 0:HALF], fin.at[0, 0:HALF], k_x + 5, xr)
    part = out_part(OWN)
    arrived(fin.at[1, 0:HALF], k_x + 2, xr)
    arrived(fin.at[1, HALF:TOK], k_x + 3, xr)
    arrived(fin.at[0, HALF:TOK], k_x + 4, xl)
    arrived(fin.at[0, 0:HALF], k_x + 5, xl)
    out_ref[...] = (part + fin[0].astype(F32) + fin[1].astype(F32)).astype(BF16)

    for cp in sends:
        cp.wait_send()
    for is_self, cp in w_copies:
        pl.when(jnp.logical_not(is_self))(cp.wait_send)

    @pl.loop(0, 4)
    def _(b):
        p_copy(b).wait_send()


N_SEM = 4 + 12 + 42 + 4 + 42 + 1 + 42 + 5 + 6


def body(keys, values, queries, step_size, gate_weight, up_weight, down_weight):
    hbm = pl.BlockSpec(memory_space=pl.ANY)
    return pl.pallas_call(
        kernel,
        out_shape=jax.ShapeDtypeStruct((TOK, DC), BF16),
        in_specs=[hbm] * 7,
        out_specs=pl.BlockSpec(memory_space=pltpu.VMEM),
        scratch_shapes=[
            pltpu.VMEM((3, PIECE, 2 * U), BF16),
            pltpu.VMEM((TOK, DC), BF16),
            pltpu.VMEM((2, TOK), F32),
            pltpu.VMEM((2, 2, PADDED, 2 * U), BF16),
            pltpu.VMEM((4, PADDED, 2 * U), BF16),
            pltpu.VMEM((NZ, 3, ROWS, U), BF16),
            pltpu.VMEM((DC, DC), BF16),
            pltpu.VMEM((DC, 3 * U), BF16),
            pltpu.VMEM((4, TOK, DC), BF16),
            pltpu.VMEM((4, TOK, DC), BF16),
            pltpu.VMEM((4, TOK, DC), BF16),
            pltpu.VMEM((DC, 4 * TOK), BF16),
            pltpu.VMEM((DC, 4 * TOK), BF16),
            pltpu.VMEM((4, TOK, 3 * U), F32),
            pltpu.VMEM((4, TOK, 3 * U), F32),
            pltpu.VMEM((2, 4 * TOK, U), BF16),
            pltpu.VMEM((4 * TOK, U), BF16),
            pltpu.VMEM((NZ, ROWS, U), F32),
            pltpu.VMEM((NZ, ROWS, U), F32),
            pltpu.VMEM((ROWS, U), BF16),
            pltpu.VMEM((NZ, ROWS, U), BF16),
            pltpu.VMEM((NZ, ROWS, U), BF16),
            pltpu.VMEM((2, 4, 2, ROWS, U), BF16),
            pltpu.VMEM((2, 4, 2, ROWS, U), BF16),
            pltpu.VMEM((ROWS, U), BF16),
            pltpu.VMEM((ROWS, U), BF16),
            pltpu.VMEM((NZ, 3, ROWS, U), BF16),
            pltpu.VMEM((8, U), F32),
            pltpu.VMEM((8, U), F32),
            pltpu.VMEM((4, TOK, 2 * U), F32),
            pltpu.VMEM((4, TOK, 2 * U), F32),
            pltpu.VMEM((4, TOK, U), BF16),
            pltpu.VMEM((4, TOK, DC), BF16),
            pltpu.VMEM((2, HALF, DC), F32),
            pltpu.VMEM((TOK, DC), BF16),
            pltpu.VMEM((2, TOK, DC), BF16),
            pltpu.SemaphoreType.DMA((N_SEM,)),
            pltpu.SemaphoreType.DMA((N_SEM,)),
            pltpu.SemaphoreType.DMA((9,)),
        ],
        compiler_params=pltpu.CompilerParams(
            collective_id=0, has_side_effects=True, vmem_limit_bytes=60 << 20
        ),
        name="ttt_layer",
    )(keys, values, queries, step_size.T, gate_weight, up_weight, down_weight)


def solution(mesh):
    finer = Mesh(mesh.devices.reshape(2, 2, 4, 2, 8), ("yh", "core", "x", "yl", "z"))
    seq, head = ("x", "yl", "z"), ("yh", "core")
    placed = (
        P(seq, head), P(seq, head), P(seq, head), P(seq, None),
        P(seq, head), P(seq, head), P(seq, head),
    )
    return jax.shard_map(body, mesh=finer, in_specs=placed, out_specs=P(seq, head), check_vma=False)
```

time: 102 us -> 92 us (0.902)
  Pallas kernels: 98.7 us -> 90.2 us
  local copies, waits for them, and re-layouts: 3.1 us -> 1.66 us
    pallas_call x1, Pallas kernels: 98.7 us -> 90.2 us  [body(): pl.pallas_call(kernel, out_shape=jax.ShapeDtypeStruct((TOK, DC), BF16), i...]
    unnamed x2 -> x1, local copies, waits for them, and re-layouts: 3.1 us -> 1.66 us
where the time goes in v2:
time: 92 us; the launch traced here: 91.9 us
  Pallas kernels  90.2 us (98%)
  local copies, waits for them, and re-layouts  1.66 us (2%)
    pallas_call x1, Pallas kernels, body(): pl.pallas_call(kernel, out_shape=jax.ShapeDtypeStruct((TOK, DC), BF16), i...  90.2 us

profile of v2, /device:TPU:1, one launch (start us, length us, event | category | flops | bytes accessed | tf_op | source)
XLA Modules:
  0.0 91.9 jit_solution(808303009031835513)
XLA Ops:
  0.0 90.2 %ttt_layer.1 = bf16[192,640]{1,0:T(8,128)(2,1)} custom-call(bf16[192,640]{1,0:T(8,128)(2,1)} %k_hbm.1, bf16[192,640]{1,0:T(8,128)(2,1)} %v_hbm.1, bf16[192,640]{1,0:T(8,128)(2,1)} %q_hbm.1, f32[2,192]{1,0:T(2,128)} %bitcast.1, bf16[20,768]{1,0:T(8,128)(2,1)} %w1_hbm.1, bf16[20,768]{1,0:T(8,128)(2,1)} %w3_hbm.1, bf16[20,768]{1,0:T(8,128)(2,1)} %w2_hbm.1), custom_call_target="tpu_custom_call" | custom-call | tf_op jit(solution)/shard_map/ttt_layer/pallas_call | solution.py:455
  90.2 1.7 %copy.9 = bf16[192,640]{1,0:T(8,128)(2,1)} copy(bf16[192,640]{1,0:T(8,128)(2,1)} %ttt_layer.1) | data formatting | bytes 491520

commit v3 on v2

--- a/solution.py
+++ b/solution.py
@@ -17,12 +17,13 @@
 U = 384
 ROWS = 80
 PIECE = 20
-PADDED = 32
+PADDED = 48
+SECOND = 24
 HALF = TOK // 2
 CUT = ((0, 48), (48, ROWS))
 CHUNKS = ((0, 0), (0, 1), (1, 0), (1, 1))
 OPP, LEFT, RIGHT, OWN = 0, 1, 2, 3
-STEP = 32
+STEP = 96
 
 
 def dot(a, b):
@@ -110,8 +111,8 @@
         loads[m].wait()
     for j in range(2):
         for t in range(2):
-            wsend[j, t, 0:PIECE, 0:U] = win[t, :, j * U:(j + 1) * U]
-            wsend[j, t, 0:PIECE, U:2 * U] = win[2, :, j * U:(j + 1) * U]
+            wsend[j, t, 0:PIECE, :] = win[t, :, j * U:(j + 1) * U]
+            wsend[j, t, SECOND:SECOND + PIECE, :] = win[2, :, j * U:(j + 1) * U]
     loads[3].wait()
     pl.semaphore_wait(barrier, 10 - jnp.where(own_w, 1, 0))
 
@@ -185,16 +186,16 @@
     prow = lax.broadcasted_iota(jnp.int32, (ROWS, 4 * PADDED), 0)
     pcol = lax.broadcasted_iota(jnp.int32, (ROWS, 4 * PADDED), 1)
     pgroup = (prow >= 20).astype(jnp.int32) + (prow >= 40).astype(jnp.int32) + (prow >= 60).astype(jnp.int32)
-    pack = jnp.where(pcol == prow + (PADDED - PIECE) * pgroup, 1.0, 0.0).astype(BF16)
-    packed = dot(pack, warr[...].reshape(4 * PADDED, 2 * U)).astype(BF16)
-    wg[z, y] = packed[:, 0:U]
-    wg[z, 2] = packed[:, U:2 * U]
+    pfrom = prow + (PADDED - PIECE) * pgroup
+    blocks = warr[...].reshape(4 * PADDED, U)
+    wg[z, 0] = dot(jnp.where(pcol == pfrom, 1.0, 0.0).astype(BF16), blocks).astype(BF16)
+    wg[z, 2] = dot(jnp.where(pcol == pfrom + SECOND, 1.0, 0.0).astype(BF16), blocks).astype(BF16)
 
     def zpos(off):
         return lax.rem(z + off + 2 * NZ, NZ)
 
     def chunk(buf, at, kind, h):
-        return buf.at[at, y if kind == 0 else 2, CUT[h][0]:CUT[h][1]]
+        return buf.at[at, 2 * kind, CUT[h][0]:CUT[h][1]]
 
     def ways(step, kind, h):
         return (0, 1) if step < 4 else (far_way(kind, h),)
@@ -218,11 +219,20 @@
     def pair_send(buf, k, step):
         for i, off in enumerate(offsets(step)):
             at = zpos(off)
-            send(buf.at[at, y], buf.at[at, y], k + 2 * step + i, ypeer)
-
-    def pair_arrived(buf, k, step):
-        for i, off in enumerate(offsets(step)):
-            arrived(buf.at[zpos(off), 1 - y], k + 2 * step + i, ypeer)
+            send(buf.at[at, 0], buf.at[at, 1], k + 2 * step + i, ypeer)
+
+    def pair_send_far(buf, k, k_ring):
+        for h in range(2):
+            ring_arrived(buf, k_ring, 4, 0, h)
+            at, rows = zpos(4), pl.ds(CUT[h][0], CUT[h][1] - CUT[h][0])
+            send(buf.at[at, 0, rows], buf.at[at, 1, rows], k + 8 + h, ypeer)
+
+    def pair_arrived(buf, k):
+        for step in range(4):
+            for i, off in enumerate(offsets(step)):
+                arrived(buf.at[zpos(off), 1], k + 2 * step + i, ypeer)
+        for h in range(2):
+            arrived(buf.at[zpos(4), 1, CUT[h][0]:CUT[h][1]], k + 8 + h, ypeer)
 
     def gather(buf, k, k_pair, step):
         for kind, h in CHUNKS:
@@ -234,26 +244,25 @@
 
     k_g, k_gp = ids(32), ids(10)
     gather(wg, k_g, k_gp, 1)
+    x_relay(kbuf, k_k)
     gather(wg, k_g, k_gp, 2)
-    x_relay(kbuf, k_k)
     gather(wg, k_g, k_gp, 3)
+    x_relay(obuf, k_o)
     gather(wg, k_g, k_gp, 4)
-    x_relay(obuf, k_o)
     loads[6].wait()
     x_out(qbuf, k_q)
-    for h in range(2):
-        ring_arrived(wg, k_g, 4, 0, h)
-    pair_send(wg, k_gp, 4)
+    pair_send_far(wg, k_gp, k_g)
+
+    def in_order(m):
+        return dot(perm[...], wg[:, m].reshape(DC, U)).astype(BF16)
+
     for h in range(2):
         ring_arrived(wg, k_g, 4, 1, h)
+    wcur[2] = in_order(2)
+    wcur[0] = in_order(0)
+    pair_arrived(wg, k_gp)
+    wcur[1] = in_order(1)
     x_last(kbuf, k_k)
-    for h in range(2):
-        kt[:, h * U:(h + 1) * U] = kbuf[2 * h:2 * h + 2].reshape(2 * TOK, DC).T
-    wcur[:, 2 * U:3 * U] = dot(perm[...], wg[:, 2].reshape(DC, U)).astype(BF16)
-    for step in range(5):
-        pair_arrived(wg, k_gp, step)
-    for m in range(2):
-        wcur[:, m * U:(m + 1) * U] = dot(perm[...], wg[:, m].reshape(DC, U)).astype(BF16)
 
     k_p = ids(4)
 
@@ -264,11 +273,13 @@
     def _(i):
         b = 3 - i
         pl.when(i == 3)(lambda: x_last(obuf, k_o))
-        ps[b, :, 0:2 * U] = dot(kbuf[b], wcur[:, 0:2 * U])
-        ps[b, :, 2 * U:3 * U] = dot(obuf[b], wcur[:, 2 * U:3 * U])
+        ps[b, 0] = dot(kbuf[b], wcur[0])
+        ps[b, 1] = dot(kbuf[b], wcur[1])
+        ps[b, 2] = dot(obuf[b], wcur[2])
         p_copy(b).start()
 
     for h in range(2):
+        kt[:, h * U:(h + 1) * U] = kbuf[2 * h:2 * h + 2].reshape(2 * TOK, DC).T
         ot[:, h * U:(h + 1) * U] = obuf[2 * h:2 * h + 2].reshape(2 * TOK, DC).T
 
     @pl.loop(0, 4)
@@ -280,9 +291,9 @@
         def _(t):
             r = pl.ds(pl.multiple_of(t * STEP, STEP), STEP)
             o = pl.ds(pl.multiple_of(b * TOK + t * STEP, STEP), STEP)
-            gate = ps[b, r, 0:U] + pr[b, r, 0:U]
-            up = ps[b, r, U:2 * U] + pr[b, r, U:2 * U]
-            hg = ps[b, r, 2 * U:3 * U] + pr[b, r, 2 * U:3 * U]
+            gate = ps[b, y, r, :] + pr[b, y, r, :]
+            up = ps[b, 1 - y, r, :] + pr[b, 1 - y, r, :]
+            hg = ps[b, 2, r, :] + pr[b, 2, r, :]
             sg = jax.nn.sigmoid(gate)
             silu = gate * sg
             hid[o, :] = (silu * up).astype(BF16)
@@ -294,12 +305,6 @@
     far = pl.ds(pl.multiple_of(zpos(4) * ROWS, 16), ROWS)
     ysf[...] = dot(kt[far, :], gg[1 - y]).astype(BF16)
     send(ysf, yrecv.at[zpos(4)], k_ya + 8, ypeer)
-    ysend[...] = dot(kt[...], gg[1 - y]).astype(BF16).reshape(NZ, ROWS, U)
-    for step in (3, 2, 1, 0):
-        for i, off in enumerate(offsets(step)):
-            at = zpos(off)
-            send(ysend.at[at], yrecv.at[at], k_ya + 2 * step + i, ypeer)
-    gb[...] = dot(ot[...], hid[...]).reshape(NZ, ROWS, U)
 
     def rs_send(step, kind, h, way):
         lo, hi = CUT[h]
@@ -316,8 +321,15 @@
             ring_id(k_r, step, kind, h, way), zr if way == 0 else zl,
         )
 
+    gb[zpos(4)] = dot(ot[far, :], hid[...])
     for h in range(2):
         rs_send(1, 1, h, far_way(1, h))
+    ysend[...] = dot(kt[...], gg[1 - y]).astype(BF16).reshape(NZ, ROWS, U)
+    for step in (3, 2, 1, 0):
+        for i, off in reversed(list(enumerate(offsets(step)))):
+            at = zpos(off)
+            send(ysend.at[at], yrecv.at[at], k_ya + 2 * step + i, ypeer)
+    gb[...] = dot(ot[...], hid[...]).reshape(NZ, ROWS, U)
     ga[...] = dot(kt[...], gg[y]).reshape(NZ, ROWS, U)
     arrived(yrecv.at[zpos(4)], k_ya + 8, ypeer)
     for h in range(2):
@@ -333,7 +345,7 @@
                 rs_send(step, 0, h, way)
         if step == 2:
             for m in range(3):
-                sms[m:m + 1, :] = square_sums(wcur[:, m * U:(m + 1) * U])
+                sms[m:m + 1, :] = square_sums(wcur[m])
         if step == 3:
             x_relay(qbuf, k_q)
 
@@ -352,59 +364,58 @@
     own_rows = pl.ds(pl.multiple_of(z * ROWS, 16), ROWS)
     arrived(yrecv.at[z], k_ya, ypeer)
     ta = total(0) + yrecv[z].astype(F32)
-    old_a = jnp.where(y == 0, wcur[own_rows, 0:U].astype(F32), wcur[own_rows, U:2 * U].astype(F32))
-    nw[z, y] = (old_a - ta).astype(BF16)
+    nw[z, 0] = (wcur[0, own_rows, :].astype(F32) - ta).astype(BF16)
     k_n, k_np = ids(32), ids(10)
     for h in range(2):
         ring_send(nw, k_n, 1, 0, h)
     pair_send(nw, k_np, 0)
     arrived(ybr, k_yb, ypeer)
-    nw[z, 2] = (wcur[own_rows, 2 * U:3 * U].astype(F32) - (gb[z] + ybr[...].astype(F32))).astype(BF16)
+    nw[z, 2] = (wcur[2, own_rows, :].astype(F32) - (gb[z] + ybr[...].astype(F32))).astype(BF16)
     for h in range(2):
         ring_send(nw, k_n, 1, 1, h)
     x_last(qbuf, k_q)
     for step in range(2, 5):
         gather(nw, k_n, k_np, step)
-    for h in range(2):
-        ring_arrived(nw, k_n, 4, 0, h)
-    pair_send(nw, k_np, 4)
+    pair_send_far(nw, k_np, k_n)
+
+    k_qp = ids(8)
+    k_s = ids(1)
+
+    def q_copy(b, kind):
+        return copy(qs.at[b, kind], qr.at[b, kind], k_qp + 2 * b + kind, peer)
+
+    def q_part(b, kind):
+        qs[b, kind] = dot(qbuf[b], nw[:, kind].reshape(DC, U))
+        cp = q_copy(b, kind)
+        cp.start()
+        sends.append(cp)
+
+    for b in range(4):
+        q_part(b, 0)
     for h in range(2):
         ring_arrived(nw, k_n, 4, 1, h)
     sms[5:6, :] = square_sums(nw[:, 2].reshape(DC, U))
-    for step in range(5):
-        pair_arrived(nw, k_np, step)
-
-    k_qp = ids(4)
-    k_s = ids(1)
-
-    def q_copy(b):
-        return copy(qs.at[b], qr.at[b], k_qp + b, peer)
-
-    def q_part(b):
-        for m in range(2):
-            qs[b, :, m * U:(m + 1) * U] = dot(qbuf[b], nw[:, m].reshape(DC, U))
-        cp = q_copy(b)
-        cp.start()
-        sends.append(cp)
-
-    q_part(OPP)
+    pair_arrived(nw, k_np)
+    q_part(OPP, 1)
     for m in range(2):
         sms[3 + m:4 + m, :] = square_sums(nw[:, m].reshape(DC, U))
     sms[6:8, :] = jnp.zeros((2, U), F32)
     send(sms, smr, k_s, peer)
-    q_part(LEFT)
+    q_part(LEFT, 1)
     arrived(smr, k_s, peer)
     sums = sms[...] + smr[...]
-    r1, r3, r2 = [jnp.sqrt((sums[m:m + 1] + EPS) / (sums[3 + m:4 + m] + EPS)) for m in range(3)]
+    ra, rb, r2 = [jnp.sqrt((sums[m:m + 1] + EPS) / (sums[3 + m:4 + m] + EPS)) for m in range(3)]
+    r1, r3 = jnp.where(y == 0, ra, rb), jnp.where(y == 0, rb, ra)
 
     def out_part(b):
-        q_copy(b).wait_recv()
+        q_copy(b, 0).wait_recv()
+        q_copy(b, 1).wait_recv()
 
         @pl.loop(0, TOK // STEP)
         def _(t):
             r = pl.ds(pl.multiple_of(t * STEP, STEP), STEP)
-            qg = (qs[b, r, 0:U] + qr[b, r, 0:U]) * r1
-            qu = (qs[b, r, U:2 * U] + qr[b, r, U:2 * U]) * r3
+            qg = (qs[b, y, r, :] + qr[b, y, r, :]) * r1
+            qu = (qs[b, 1 - y, r, :] + qr[b, 1 - y, r, :]) * r3
             qh[b, r, :] = (qg * jax.nn.sigmoid(qg) * qu * r2).astype(BF16)
 
         return dot_nt(qh[b], nw[:, 2].reshape(DC, U))
@@ -414,12 +425,12 @@
     ob[OPP] = part.astype(BF16)
     send(ob.at[OPP, 0:HALF], obr.at[0:HALF], k_x, xr)
     send(ob.at[OPP, HALF:TOK], obr.at[HALF:TOK], k_x + 1, xl)
-    q_part(RIGHT)
+    q_part(RIGHT, 1)
     part = out_part(LEFT)
     ob[LEFT, 0:HALF] = part[0:HALF].astype(BF16)
     send(ob.at[LEFT, 0:HALF], fin.at[1, 0:HALF], k_x + 2, xl)
     op[0] = part[HALF:TOK]
-    q_part(OWN)
+    q_part(OWN, 1)
     part = out_part(RIGHT)
     ob[RIGHT, HALF:TOK] = part[HALF:TOK].astype(BF16)
     send(ob.at[RIGHT, HALF:TOK], fin.at[0, HALF:TOK], k_x + 4, xr)
@@ -447,7 +458,7 @@
         p_copy(b).wait_send()
 
 
-N_SEM = 4 + 12 + 42 + 4 + 42 + 1 + 42 + 5 + 6
+N_SEM = 4 + 12 + 42 + 4 + 42 + 1 + 42 + 9 + 6
 
 
 def body(keys, values, queries, step_size, gate_weight, up_weight, down_weight):
@@ -461,18 +472,18 @@
             pltpu.VMEM((3, PIECE, 2 * U), BF16),
             pltpu.VMEM((TOK, DC), BF16),
             pltpu.VMEM((2, TOK), F32),
-            pltpu.VMEM((2, 2, PADDED, 2 * U), BF16),
-            pltpu.VMEM((4, PADDED, 2 * U), BF16),
+            pltpu.VMEM((2, 2, PADDED, U), BF16),
+            pltpu.VMEM((4, PADDED, U), BF16),
             pltpu.VMEM((NZ, 3, ROWS, U), BF16),
             pltpu.VMEM((DC, DC), BF16),
-            pltpu.VMEM((DC, 3 * U), BF16),
+            pltpu.VMEM((3, DC, U), BF16),
             pltpu.VMEM((4, TOK, DC), BF16),
             pltpu.VMEM((4, TOK, DC), BF16),
             pltpu.VMEM((4, TOK, DC), BF16),
             pltpu.VMEM((DC, 4 * TOK), BF16),
             pltpu.VMEM((DC, 4 * TOK), BF16),
-            pltpu.VMEM((4, TOK, 3 * U), F32),
-            pltpu.VMEM((4, TOK, 3 * U), F32),
+            pltpu.VMEM((4, 3, TOK, U), F32),
+            pltpu.VMEM((4, 3, TOK, U), F32),
             pltpu.VMEM((2, 4 * TOK, U), BF16),
             pltpu.VMEM((4 * TOK, U), BF16),
             pltpu.VMEM((NZ, ROWS, U), F32),
@@ -487,8 +498,8 @@
             pltpu.VMEM((NZ, 3, ROWS, U), BF16),
             pltpu.VMEM((8, U), F32),
             pltpu.VMEM((8, U), F32),
-            pltpu.VMEM((4, TOK, 2 * U), F32),
-            pltpu.VMEM((4, TOK, 2 * U), F32),
+            pltpu.VMEM((4, 2, TOK, U), F32),
+            pltpu.VMEM((4, 2, TOK, U), F32),
             pltpu.VMEM((4, TOK, U), BF16),
             pltpu.VMEM((4, TOK, DC), BF16),
             pltpu.VMEM((2, HALF, DC), F32),

time: 92 us -> 92 us (level)
  no operation moved by 1% of the time
where the time goes in v3:
time: 92 us; the launch traced here: 91.9 us
  Pallas kernels  90.2 us (98%)
  local copies, waits for them, and re-layouts  1.66 us (2%)
    pallas_call x1, Pallas kernels, body(): pl.pallas_call(kernel, out_shape=jax.ShapeDtypeStruct((TOK, DC), BF16), i...  90.2 us

profile of v3, /device:TPU:1, one launch (start us, length us, event | category | flops | bytes accessed | tf_op | source)
XLA Modules:
  0.0 91.9 jit_solution(11243356972361662020)
XLA Ops:
  0.0 90.2 %ttt_layer.1 = bf16[192,640]{1,0:T(8,128)(2,1)} custom-call(bf16[192,640]{1,0:T(8,128)(2,1)} %k_hbm.1, bf16[192,640]{1,0:T(8,128)(2,1)} %v_hbm.1, bf16[192,640]{1,0:T(8,128)(2,1)} %q_hbm.1, f32[2,192]{1,0:T(2,128)} %bitcast.1, bf16[20,768]{1,0:T(8,128)(2,1)} %w1_hbm.1, bf16[20,768]{1,0:T(8,128)(2,1)} %w3_hbm.1, bf16[20,768]{1,0:T(8,128)(2,1)} %w2_hbm.1), custom_call_target="tpu_custom_call" | custom-call | tf_op jit(solution)/shard_map/ttt_layer/pallas_call | solution.py:466
  90.3 1.7 %copy.9 = bf16[192,640]{1,0:T(8,128)(2,1)} copy(bf16[192,640]{1,0:T(8,128)(2,1)} %ttt_layer.1) | data formatting | bytes 491520

commit v4 on v3

--- a/solution.py
+++ b/solution.py
@@ -45,8 +45,8 @@
 
 def kernel(
     k_hbm, v_hbm, q_hbm, s_hbm, w1_hbm, w3_hbm, w2_hbm, out_ref,
-    win, vin, sin, wsend, warr, wg, perm, wcur, kbuf, obuf, qbuf, kt, ot, ps, pr, gg, hid,
-    ga, gb, ysf, ysend, yrecv, rss, rsr, ybs, ybr, nw, sms, smr, qs, qr, qh, ob, op, obr, fin,
+    win, kin, vin, qin, sin, wsend, warr, wg, perm, wout, kbuf, obuf, qbuf, kt, ot, ps, pb, pr, gg, hid,
+    ga, gb, ysf, ysend, yrecv, rss, rsr, ybs, ybr, nw, sms, smr, qs, qb, qr, qh, ob, op, obr, fin,
     send_sem, recv_sem, loc_sem,
 ):
     yh = lax.axis_index("yh")
@@ -98,10 +98,10 @@
         pltpu.make_async_copy(w1_hbm, win.at[0], loc_sem.at[0]),
         pltpu.make_async_copy(w3_hbm, win.at[1], loc_sem.at[1]),
         pltpu.make_async_copy(w2_hbm, win.at[2], loc_sem.at[2]),
-        pltpu.make_async_copy(k_hbm, kbuf.at[OWN], loc_sem.at[3]),
+        pltpu.make_async_copy(k_hbm, kin, loc_sem.at[3]),
         pltpu.make_async_copy(v_hbm, vin, loc_sem.at[4]),
         pltpu.make_async_copy(s_hbm, sin, loc_sem.at[5]),
-        pltpu.make_async_copy(q_hbm, qbuf.at[OWN], loc_sem.at[6]),
+        pltpu.make_async_copy(q_hbm, qin, loc_sem.at[6]),
     ]
     for ld in loads:
         ld.start()
@@ -113,7 +113,21 @@
         for t in range(2):
             wsend[j, t, 0:PIECE, :] = win[t, :, j * U:(j + 1) * U]
             wsend[j, t, SECOND:SECOND + PIECE, :] = win[2, :, j * U:(j + 1) * U]
+    row = lax.broadcasted_iota(jnp.int32, (DC, DC), 0)
+    col = lax.broadcasted_iota(jnp.int32, (DC, DC), 1)
+    group = (row >= 160).astype(jnp.int32) + (row >= 320).astype(jnp.int32) + (row >= 480).astype(jnp.int32)
+    rem = row - 160 * group
+    step20 = jnp.zeros_like(rem)
+    for t in range(1, NZ):
+        step20 = step20 + (rem >= PIECE * t).astype(jnp.int32)
+    wanted = ROWS * step20 + PIECE * group + rem - PIECE * step20
+    perm[...] = jnp.where(col == wanted, 1.0, 0.0).astype(BF16)
+
+    def gathered_order(v):
+        return dot(v, perm[...]).astype(BF16)
+
     loads[3].wait()
+    kbuf[OWN] = gathered_order(kin[...])
     pl.semaphore_wait(barrier, 10 - jnp.where(own_w, 1, 0))
 
     k_w = ids(4)
@@ -162,18 +176,10 @@
     diag = lax.broadcasted_iota(jnp.int32, (TOK, TOK), 0) == lax.broadcasted_iota(jnp.int32, (TOK, TOK), 1)
     rate_row = jnp.where(yh == 0, sin[0:1, :], sin[1:2, :])
     rates = jnp.sum(jnp.where(diag, rate_row, 0.0), axis=1, keepdims=True)
-    obuf[OWN] = (-(rates * vin[...].astype(F32))).astype(BF16)
+    obuf[OWN] = gathered_order((-(rates * vin[...].astype(F32))).astype(BF16))
     x_out(obuf, k_o)
-
-    row = lax.broadcasted_iota(jnp.int32, (DC, DC), 0)
-    col = lax.broadcasted_iota(jnp.int32, (DC, DC), 1)
-    group = (row >= 160).astype(jnp.int32) + (row >= 320).astype(jnp.int32) + (row >= 480).astype(jnp.int32)
-    rem = row - 160 * group
-    step20 = jnp.zeros_like(rem)
-    for t in range(1, NZ):
-        step20 = step20 + (rem >= PIECE * t).astype(jnp.int32)
-    wanted = ROWS * step20 + PIECE * group + rem - PIECE * step20
-    perm[...] = jnp.where(col == wanted, 1.0, 0.0).astype(BF16)
+    loads[6].wait()
+    qbuf[OWN] = gathered_order(qin[...])
 
     for s in range(4):
         from_x, from_y = s // 2, s % 2
@@ -244,56 +250,50 @@
 
     k_g, k_gp = ids(32), ids(10)
     gather(wg, k_g, k_gp, 1)
-    x_relay(kbuf, k_k)
     gather(wg, k_g, k_gp, 2)
     gather(wg, k_g, k_gp, 3)
+    x_relay(kbuf, k_k)
+    gather(wg, k_g, k_gp, 4)
     x_relay(obuf, k_o)
-    gather(wg, k_g, k_gp, 4)
-    loads[6].wait()
     x_out(qbuf, k_q)
     pair_send_far(wg, k_gp, k_g)
 
-    def in_order(m):
-        return dot(perm[...], wg[:, m].reshape(DC, U)).astype(BF16)
-
     for h in range(2):
         ring_arrived(wg, k_g, 4, 1, h)
-    wcur[2] = in_order(2)
-    wcur[0] = in_order(0)
+    k_p = ids(12)
+
+    def p_part(b, kind):
+        v = dot((obuf if kind == 2 else kbuf)[b], wg[:, kind].reshape(DC, U))
+        ps[b, kind] = v
+        pb[b, kind] = v.astype(BF16)
+        send(pb.at[b, kind], pr.at[b, kind], k_p + 3 * b + kind, peer)
+
+    for b in (OWN, RIGHT, LEFT):
+        p_part(b, 0)
+        p_part(b, 2)
+    x_last(kbuf, k_k)
+    p_part(OPP, 0)
+    x_last(obuf, k_o)
+    p_part(OPP, 2)
     pair_arrived(wg, k_gp)
-    wcur[1] = in_order(1)
-    x_last(kbuf, k_k)
-
-    k_p = ids(4)
-
-    def p_copy(b):
-        return copy(ps.at[b], pr.at[b], k_p + b, peer)
-
-    @pl.loop(0, 4)
-    def _(i):
-        b = 3 - i
-        pl.when(i == 3)(lambda: x_last(obuf, k_o))
-        ps[b, 0] = dot(kbuf[b], wcur[0])
-        ps[b, 1] = dot(kbuf[b], wcur[1])
-        ps[b, 2] = dot(obuf[b], wcur[2])
-        p_copy(b).start()
+    for b in (OWN, RIGHT, LEFT, OPP):
+        p_part(b, 1)
 
     for h in range(2):
         kt[:, h * U:(h + 1) * U] = kbuf[2 * h:2 * h + 2].reshape(2 * TOK, DC).T
         ot[:, h * U:(h + 1) * U] = obuf[2 * h:2 * h + 2].reshape(2 * TOK, DC).T
 
-    @pl.loop(0, 4)
-    def _(i):
-        b = 3 - i
-        p_copy(b).wait_recv()
+    for b in (OWN, RIGHT, LEFT, OPP):
+        for kind in range(3):
+            arrived(pr.at[b, kind], k_p + 3 * b + kind, peer)
 
         @pl.loop(0, TOK // STEP)
         def _(t):
             r = pl.ds(pl.multiple_of(t * STEP, STEP), STEP)
             o = pl.ds(pl.multiple_of(b * TOK + t * STEP, STEP), STEP)
-            gate = ps[b, y, r, :] + pr[b, y, r, :]
-            up = ps[b, 1 - y, r, :] + pr[b, 1 - y, r, :]
-            hg = ps[b, 2, r, :] + pr[b, 2, r, :]
+            gate = ps[b, y, r, :] + pr[b, y, r, :].astype(F32)
+            up = ps[b, 1 - y, r, :] + pr[b, 1 - y, r, :].astype(F32)
+            hg = ps[b, 2, r, :] + pr[b, 2, r, :].astype(F32)
             sg = jax.nn.sigmoid(gate)
             silu = gate * sg
             hid[o, :] = (silu * up).astype(BF16)
@@ -345,7 +345,7 @@
                 rs_send(step, 0, h, way)
         if step == 2:
             for m in range(3):
-                sms[m:m + 1, :] = square_sums(wcur[m])
+                sms[m:m + 1, :] = square_sums(wg[:, m].reshape(DC, U))
         if step == 3:
             x_relay(qbuf, k_q)
 
@@ -361,16 +361,15 @@
     gb[z] = tb
     ybs[...] = tb.astype(BF16)
     send(ybs, ybr, k_yb, ypeer)
-    own_rows = pl.ds(pl.multiple_of(z * ROWS, 16), ROWS)
     arrived(yrecv.at[z], k_ya, ypeer)
     ta = total(0) + yrecv[z].astype(F32)
-    nw[z, 0] = (wcur[0, own_rows, :].astype(F32) - ta).astype(BF16)
+    nw[z, 0] = (wg[z, 0].astype(F32) - ta).astype(BF16)
     k_n, k_np = ids(32), ids(10)
     for h in range(2):
         ring_send(nw, k_n, 1, 0, h)
     pair_send(nw, k_np, 0)
     arrived(ybr, k_yb, ypeer)
-    nw[z, 2] = (wcur[2, own_rows, :].astype(F32) - (gb[z] + ybr[...].astype(F32))).astype(BF16)
+    nw[z, 2] = (wg[z, 2].astype(F32) - (gb[z] + ybr[...].astype(F32))).astype(BF16)
     for h in range(2):
         ring_send(nw, k_n, 1, 1, h)
     x_last(qbuf, k_q)
@@ -381,20 +380,18 @@
     k_qp = ids(8)
     k_s = ids(1)
 
-    def q_copy(b, kind):
-        return copy(qs.at[b, kind], qr.at[b, kind], k_qp + 2 * b + kind, peer)
-
     def q_part(b, kind):
-        qs[b, kind] = dot(qbuf[b], nw[:, kind].reshape(DC, U))
-        cp = q_copy(b, kind)
-        cp.start()
-        sends.append(cp)
+        v = dot(qbuf[b], nw[:, kind].reshape(DC, U))
+        qs[b, kind] = v
+        qb[b, kind] = v.astype(BF16)
+        send(qb.at[b, kind], qr.at[b, kind], k_qp + 2 * b + kind, peer)
 
     for b in range(4):
         q_part(b, 0)
     for h in range(2):
         ring_arrived(nw, k_n, 4, 1, h)
     sms[5:6, :] = square_sums(nw[:, 2].reshape(DC, U))
+    wout[...] = dot(perm[...], nw[:, 2].reshape(DC, U)).astype(BF16)
     pair_arrived(nw, k_np)
     q_part(OPP, 1)
     for m in range(2):
@@ -408,17 +405,17 @@
     r1, r3 = jnp.where(y == 0, ra, rb), jnp.where(y == 0, rb, ra)
 
     def out_part(b):
-        q_copy(b, 0).wait_recv()
-        q_copy(b, 1).wait_recv()
+        for kind in range(2):
+            arrived(qr.at[b, kind], k_qp + 2 * b + kind, peer)
 
         @pl.loop(0, TOK // STEP)
         def _(t):
             r = pl.ds(pl.multiple_of(t * STEP, STEP), STEP)
-            qg = (qs[b, y, r, :] + qr[b, y, r, :]) * r1
-            qu = (qs[b, 1 - y, r, :] + qr[b, 1 - y, r, :]) * r3
+            qg = (qs[b, y, r, :] + qr[b, y, r, :].astype(F32)) * r1
+            qu = (qs[b, 1 - y, r, :] + qr[b, 1 - y, r, :].astype(F32)) * r3
             qh[b, r, :] = (qg * jax.nn.sigmoid(qg) * qu * r2).astype(BF16)
 
-        return dot_nt(qh[b], nw[:, 2].reshape(DC, U))
+        return dot_nt(qh[b], wout[...])
 
     k_x = ids(6)
     part = out_part(OPP)
@@ -453,12 +450,8 @@
     for is_self, cp in w_copies:
         pl.when(jnp.logical_not(is_self))(cp.wait_send)
 
-    @pl.loop(0, 4)
-    def _(b):
-        p_copy(b).wait_send()
-
-
-N_SEM = 4 + 12 + 42 + 4 + 42 + 1 + 42 + 9 + 6
+
+N_SEM = 4 + 12 + 42 + 12 + 42 + 1 + 42 + 9 + 6
 
 
 def body(keys, values, queries, step_size, gate_weight, up_weight, down_weight):
@@ -471,19 +464,22 @@
         scratch_shapes=[
             pltpu.VMEM((3, PIECE, 2 * U), BF16),
             pltpu.VMEM((TOK, DC), BF16),
+            pltpu.VMEM((TOK, DC), BF16),
+            pltpu.VMEM((TOK, DC), BF16),
             pltpu.VMEM((2, TOK), F32),
             pltpu.VMEM((2, 2, PADDED, U), BF16),
             pltpu.VMEM((4, PADDED, U), BF16),
             pltpu.VMEM((NZ, 3, ROWS, U), BF16),
             pltpu.VMEM((DC, DC), BF16),
-            pltpu.VMEM((3, DC, U), BF16),
+            pltpu.VMEM((DC, U), BF16),
             pltpu.VMEM((4, TOK, DC), BF16),
             pltpu.VMEM((4, TOK, DC), BF16),
             pltpu.VMEM((4, TOK, DC), BF16),
             pltpu.VMEM((DC, 4 * TOK), BF16),
             pltpu.VMEM((DC, 4 * TOK), BF16),
             pltpu.VMEM((4, 3, TOK, U), F32),
-            pltpu.VMEM((4, 3, TOK, U), F32),
+            pltpu.VMEM((4, 3, TOK, U), BF16),
+            pltpu.VMEM((4, 3, TOK, U), BF16),
             pltpu.VMEM((2, 4 * TOK, U), BF16),
             pltpu.VMEM((4 * TOK, U), BF16),
             pltpu.VMEM((NZ, ROWS, U), F32),
@@ -499,7 +495,8 @@
             pltpu.VMEM((8, U), F32),
             pltpu.VMEM((8, U), F32),
             pltpu.VMEM((4, 2, TOK, U), F32),
-            pltpu.VMEM((4, 2, TOK, U), F32),
+            pltpu.VMEM((4, 2, TOK, U), BF16),
+            pltpu.VMEM((4, 2, TOK, U), BF16),
             pltpu.VMEM((4, TOK, U), BF16),
             pltpu.VMEM((4, TOK, DC), BF16),
             pltpu.VMEM((2, HALF, DC), F32),

time: 92 us -> 90.1 us (0.979)
  Pallas kernels: 90.2 us -> 88.3 us
    pallas_call x1, Pallas kernels: 90.2 us -> 88.3 us  [body(): pl.pallas_call(kernel, out_shape=jax.ShapeDtypeStruct((TOK, DC), BF16), i...]
where the time goes in v4:
time: 90.1 us; the launch traced here: 89.9 us
  Pallas kernels  88.3 us (98%)
  local copies, waits for them, and re-layouts  1.66 us (2%)
    pallas_call x1, Pallas kernels, body(): pl.pallas_call(kernel, out_shape=jax.ShapeDtypeStruct((TOK, DC), BF16), i...  88.3 us

profile of v4, /device:TPU:1, one launch (start us, length us, event | category | flops | bytes accessed | tf_op | source)
XLA Modules:
  0.0 89.9 jit_solution(6969775960654373992)
XLA Ops:
  0.0 88.3 %ttt_layer.1 = bf16[192,640]{1,0:T(8,128)(2,1)} custom-call(bf16[192,640]{1,0:T(8,128)(2,1)} %k_hbm.1, bf16[192,640]{1,0:T(8,128)(2,1)} %v_hbm.1, bf16[192,640]{1,0:T(8,128)(2,1)} %q_hbm.1, f32[2,192]{1,0:T(2,128)} %bitcast.1, bf16[20,768]{1,0:T(8,128)(2,1)} %w1_hbm.1, bf16[20,768]{1,0:T(8,128)(2,1)} %w3_hbm.1, bf16[20,768]{1,0:T(8,128)(2,1)} %w2_hbm.1), custom_call_target="tpu_custom_call" | custom-call | tf_op jit(solution)/shard_map/ttt_layer/pallas_call | solution.py:459
  88.3 1.7 %copy.9 = bf16[192,640]{1,0:T(8,128)(2,1)} copy(bf16[192,640]{1,0:T(8,128)(2,1)} %ttt_layer.1) | data formatting | bytes 491520

commit v5 on v4

--- a/solution.py
+++ b/solution.py
@@ -46,7 +46,7 @@
 def kernel(
     k_hbm, v_hbm, q_hbm, s_hbm, w1_hbm, w3_hbm, w2_hbm, out_ref,
     win, kin, vin, qin, sin, wsend, warr, wg, perm, wout, kbuf, obuf, qbuf, kt, ot, ps, pb, pr, gg, hid,
-    ga, gb, ysf, ysend, yrecv, rss, rsr, ybs, ybr, nw, sms, smr, qs, qb, qr, qh, ob, op, obr, fin,
+    ga, gb, yfar, ysend, yrecv, rss, rsr, ybs, ybr, nw, sms, smr, qs, qr, qh, ob, op, obr, fin,
     send_sem, recv_sem, loc_sem,
 ):
     yh = lax.axis_index("yh")
@@ -56,6 +56,7 @@
     z = lax.axis_index("z")
     xr, xl = {"x": lax.rem(x + 1, NX)}, {"x": lax.rem(x + NX - 1, NX)}
     zr, zl = {"z": lax.rem(z + 1, NZ)}, {"z": lax.rem(z + NZ - 1, NZ)}
+    dr, dl = {"yl": 1 - y, **zr}, {"yl": 1 - y, **zl}
     peer, ypeer = {"core": 1 - c}, {"yl": 1 - y}
     xhalf = x // 2
     xlow = lax.rem(x, 2)
@@ -87,7 +88,7 @@
         copy(ref, ref, k, frm).wait_recv()
 
     barrier = pltpu.get_barrier_semaphore()
-    for to in (peer, xr, xl, zr, zl, ypeer, wtarget(0, 1), wtarget(1, 1)):
+    for to in (peer, xr, xl, zr, zl, dr, dl, ypeer, wtarget(0, 1), wtarget(1, 1)):
         pl.semaphore_signal(barrier, inc=1, device_id=to, device_id_type=MESH)
     for j in range(2):
         @pl.when(jnp.logical_not(jnp.logical_and(own_w, xlow == j)))
@@ -128,7 +129,7 @@
 
     loads[3].wait()
     kbuf[OWN] = gathered_order(kin[...])
-    pl.semaphore_wait(barrier, 10 - jnp.where(own_w, 1, 0))
+    pl.semaphore_wait(barrier, 12 - jnp.where(own_w, 1, 0))
 
     k_w = ids(4)
     slot = 2 * xlow + y
@@ -227,11 +228,13 @@
             at = zpos(off)
             send(buf.at[at, 0], buf.at[at, 1], k + 2 * step + i, ypeer)
 
-    def pair_send_far(buf, k, k_ring):
+    def far_send(buf, k, h):
+        at, rows = zpos(-3 if h == 0 else 3), pl.ds(CUT[h][0], CUT[h][1] - CUT[h][0])
+        send(buf.at[at, 0, rows], buf.at[at, 1, rows], k + 8 + h, dr if h == 0 else dl)
+
+    def far_arrived(buf, k):
         for h in range(2):
-            ring_arrived(buf, k_ring, 4, 0, h)
-            at, rows = zpos(4), pl.ds(CUT[h][0], CUT[h][1] - CUT[h][0])
-            send(buf.at[at, 0, rows], buf.at[at, 1, rows], k + 8 + h, ypeer)
+            ring_arrived(buf, k, 4, 0, h)
 
     def pair_arrived(buf, k):
         for step in range(4):
@@ -245,6 +248,8 @@
             if step > 1:
                 ring_arrived(buf, k, step - 1, kind, h)
             ring_send(buf, k, step, kind, h)
+            if step == 4 and kind == 0:
+                far_send(buf, k_pair, h)
             if (kind, h) == (0, 1):
                 pair_send(buf, k_pair, step - 1)
 
@@ -256,7 +261,7 @@
     gather(wg, k_g, k_gp, 4)
     x_relay(obuf, k_o)
     x_out(qbuf, k_q)
-    pair_send_far(wg, k_gp, k_g)
+    far_arrived(wg, k_g)
 
     for h in range(2):
         ring_arrived(wg, k_g, 4, 1, h)
@@ -303,15 +308,15 @@
     k_ya = ids(10)
     k_r = ids(32)
     far = pl.ds(pl.multiple_of(zpos(4) * ROWS, 16), ROWS)
-    ysf[...] = dot(kt[far, :], gg[1 - y]).astype(BF16)
-    send(ysf, yrecv.at[zpos(4)], k_ya + 8, ypeer)
-
     def rs_send(step, kind, h, way):
         lo, hi = CUT[h]
         at = zpos((5 - step) if way == 0 else (step - 5))
         v = (ga if kind == 0 else gb)[at, lo:hi]
-        if kind == 0:
+        if kind == 0 and step > 1:
             v = v + yrecv[at, lo:hi].astype(F32)
+        if kind == 0 and step == 2 and h == way:
+            arrived(yfar.at[lo:hi], k_ya + 8 + h, dl if way == 0 else dr)
+            v = v + yfar[lo:hi].astype(F32)
         if step > 2 or (step == 2 and far_way(kind, h) == way):
             arrived(rsr.at[way, step - 2, kind, lo:hi], ring_id(k_r, step - 1, kind, h, way), zl if way == 0 else zr)
             v = v + rsr[way, step - 2, kind, lo:hi].astype(F32)
@@ -325,15 +330,18 @@
     for h in range(2):
         rs_send(1, 1, h, far_way(1, h))
     ysend[...] = dot(kt[...], gg[1 - y]).astype(BF16).reshape(NZ, ROWS, U)
+    for h in range(2):
+        lo, hi = CUT[h]
+        send(ysend.at[zpos(4), lo:hi], yfar.at[lo:hi], k_ya + 8 + h, dr if h == 0 else dl)
     for step in (3, 2, 1, 0):
         for i, off in reversed(list(enumerate(offsets(step)))):
             at = zpos(off)
             send(ysend.at[at], yrecv.at[at], k_ya + 2 * step + i, ypeer)
+    ga[zpos(4)] = dot(kt[far, :], gg[y])
+    for h in range(2):
+        rs_send(1, 0, h, far_way(0, h))
     gb[...] = dot(ot[...], hid[...]).reshape(NZ, ROWS, U)
     ga[...] = dot(kt[...], gg[y]).reshape(NZ, ROWS, U)
-    arrived(yrecv.at[zpos(4)], k_ya + 8, ypeer)
-    for h in range(2):
-        rs_send(1, 0, h, far_way(0, h))
 
     for step in range(2, 5):
         for way in range(2):
@@ -375,16 +383,14 @@
     x_last(qbuf, k_q)
     for step in range(2, 5):
         gather(nw, k_n, k_np, step)
-    pair_send_far(nw, k_np, k_n)
+    far_arrived(nw, k_n)
 
     k_qp = ids(8)
     k_s = ids(1)
 
     def q_part(b, kind):
-        v = dot(qbuf[b], nw[:, kind].reshape(DC, U))
-        qs[b, kind] = v
-        qb[b, kind] = v.astype(BF16)
-        send(qb.at[b, kind], qr.at[b, kind], k_qp + 2 * b + kind, peer)
+        qs[b, kind] = dot(qbuf[b], nw[:, kind].reshape(DC, U))
+        send(qs.at[b, kind], qr.at[b, kind], k_qp + 2 * b + kind, peer)
 
     for b in range(4):
         q_part(b, 0)
@@ -411,8 +417,8 @@
         @pl.loop(0, TOK // STEP)
         def _(t):
             r = pl.ds(pl.multiple_of(t * STEP, STEP), STEP)
-            qg = (qs[b, y, r, :] + qr[b, y, r, :].astype(F32)) * r1
-            qu = (qs[b, 1 - y, r, :] + qr[b, 1 - y, r, :].astype(F32)) * r3
+            qg = (qs[b, y, r, :] + qr[b, y, r, :]) * r1
+            qu = (qs[b, 1 - y, r, :] + qr[b, 1 - y, r, :]) * r3
             qh[b, r, :] = (qg * jax.nn.sigmoid(qg) * qu * r2).astype(BF16)
 
         return dot_nt(qh[b], wout[...])
@@ -495,8 +501,7 @@
             pltpu.VMEM((8, U), F32),
             pltpu.VMEM((8, U), F32),
             pltpu.VMEM((4, 2, TOK, U), F32),
-            pltpu.VMEM((4, 2, TOK, U), BF16),
-            pltpu.VMEM((4, 2, TOK, U), BF16),
+            pltpu.VMEM((4, 2, TOK, U), F32),
             pltpu.VMEM((4, TOK, U), BF16),
             pltpu.VMEM((4, TOK, DC), BF16),
             pltpu.VMEM((2, HALF, DC), F32),

time: 90.1 us -> 87.8 us (0.974)
  Pallas kernels: 88.3 us -> 86 us
    pallas_call x1, Pallas kernels: 88.3 us -> 86 us  [body(): pl.pallas_call(kernel, out_shape=jax.ShapeDtypeStruct((TOK, DC), BF16), i...]
where the time goes in v5:
time: 87.8 us; the launch traced here: 87.6 us
  Pallas kernels  86 us (98%)
  local copies, waits for them, and re-layouts  1.66 us (2%)
    pallas_call x1, Pallas kernels, body(): pl.pallas_call(kernel, out_shape=jax.ShapeDtypeStruct((TOK, DC), BF16), i...  86 us

profile of v5, /device:TPU:1, one launch (start us, length us, event | category | flops | bytes accessed | tf_op | source)
XLA Modules:
  0.0 87.6 jit_solution(650752278710033333)
XLA Ops:
  0.0 86.0 %ttt_layer.1 = bf16[192,640]{1,0:T(8,128)(2,1)} custom-call(bf16[192,640]{1,0:T(8,128)(2,1)} %k_hbm.1, bf16[192,640]{1,0:T(8,128)(2,1)} %v_hbm.1, bf16[192,640]{1,0:T(8,128)(2,1)} %q_hbm.1, f32[2,192]{1,0:T(2,128)} %bitcast.1, bf16[20,768]{1,0:T(8,128)(2,1)} %w1_hbm.1, bf16[20,768]{1,0:T(8,128)(2,1)} %w3_hbm.1, bf16[20,768]{1,0:T(8,128)(2,1)} %w2_hbm.1), custom_call_target="tpu_custom_call" | custom-call | tf_op jit(solution)/shard_map/ttt_layer/pallas_call | solution.py:465
  86.0 1.7 %copy.9 = bf16[192,640]{1,0:T(8,128)(2,1)} copy(bf16[192,640]{1,0:T(8,128)(2,1)} %ttt_layer.1) | data formatting | bytes 491520

commit v6 on v5

--- a/solution.py
+++ b/solution.py
@@ -256,11 +256,17 @@
     k_g, k_gp = ids(32), ids(10)
     gather(wg, k_g, k_gp, 1)
     gather(wg, k_g, k_gp, 2)
+    x_relay(kbuf, k_k)
     gather(wg, k_g, k_gp, 3)
-    x_relay(kbuf, k_k)
+    x_relay(obuf, k_o)
     gather(wg, k_g, k_gp, 4)
-    x_relay(obuf, k_o)
     x_out(qbuf, k_q)
+
+    def transposes(h):
+        kt[:, h * U:(h + 1) * U] = kbuf[2 * h:2 * h + 2].reshape(2 * TOK, DC).T
+        ot[:, h * U:(h + 1) * U] = obuf[2 * h:2 * h + 2].reshape(2 * TOK, DC).T
+
+    transposes(1)
     far_arrived(wg, k_g)
 
     for h in range(2):
@@ -284,9 +290,7 @@
     for b in (OWN, RIGHT, LEFT, OPP):
         p_part(b, 1)
 
-    for h in range(2):
-        kt[:, h * U:(h + 1) * U] = kbuf[2 * h:2 * h + 2].reshape(2 * TOK, DC).T
-        ot[:, h * U:(h + 1) * U] = obuf[2 * h:2 * h + 2].reshape(2 * TOK, DC).T
+    transposes(0)
 
     for b in (OWN, RIGHT, LEFT, OPP):
         for kind in range(3):
@@ -396,13 +400,13 @@
         q_part(b, 0)
     for h in range(2):
         ring_arrived(nw, k_n, 4, 1, h)
+    sms[3:4, :] = square_sums(nw[:, 0].reshape(DC, U))
     sms[5:6, :] = square_sums(nw[:, 2].reshape(DC, U))
+    sms[6:8, :] = jnp.zeros((2, U), F32)
     wout[...] = dot(perm[...], nw[:, 2].reshape(DC, U)).astype(BF16)
     pair_arrived(nw, k_np)
     q_part(OPP, 1)
-    for m in range(2):
-        sms[3 + m:4 + m, :] = square_sums(nw[:, m].reshape(DC, U))
-    sms[6:8, :] = jnp.zeros((2, U), F32)
+    sms[4:5, :] = square_sums(nw[:, 1].reshape(DC, U))
     send(sms, smr, k_s, peer)
     q_part(LEFT, 1)
     arrived(smr, k_s, peer)

time: 87.8 us -> 87.1 us (level)
  no operation moved by 1% of the time
where the time goes in v6:
time: 87.1 us; the launch traced here: 87 us
  Pallas kernels  85.3 us (98%)
  local copies, waits for them, and re-layouts  1.66 us (2%)
    pallas_call x1, Pallas kernels, body(): pl.pallas_call(kernel, out_shape=jax.ShapeDtypeStruct((TOK, DC), BF16), i...  85.3 us

profile of v6, /device:TPU:1, one launch (start us, length us, event | category | flops | bytes accessed | tf_op | source)
XLA Modules:
  0.0 87.0 jit_solution(4350595010205015020)
XLA Ops:
  0.0 85.3 %ttt_layer.1 = bf16[192,640]{1,0:T(8,128)(2,1)} custom-call(bf16[192,640]{1,0:T(8,128)(2,1)} %k_hbm.1, bf16[192,640]{1,0:T(8,128)(2,1)} %v_hbm.1, bf16[192,640]{1,0:T(8,128)(2,1)} %q_hbm.1, f32[2,192]{1,0:T(2,128)} %bitcast.1, bf16[20,768]{1,0:T(8,128)(2,1)} %w1_hbm.1, bf16[20,768]{1,0:T(8,128)(2,1)} %w3_hbm.1, bf16[20,768]{1,0:T(8,128)(2,1)} %w2_hbm.1), custom_call_target="tpu_custom_call" | custom-call | tf_op jit(solution)/shard_map/ttt_layer/pallas_call | solution.py:469
  85.3 1.7 %copy.9 = bf16[192,640]{1,0:T(8,128)(2,1)} copy(bf16[192,640]{1,0:T(8,128)(2,1)} %ttt_layer.1) | data formatting | bytes 491520

commit v7 on v6

--- a/solution.py
+++ b/solution.py
@@ -114,21 +114,6 @@
         for t in range(2):
             wsend[j, t, 0:PIECE, :] = win[t, :, j * U:(j + 1) * U]
             wsend[j, t, SECOND:SECOND + PIECE, :] = win[2, :, j * U:(j + 1) * U]
-    row = lax.broadcasted_iota(jnp.int32, (DC, DC), 0)
-    col = lax.broadcasted_iota(jnp.int32, (DC, DC), 1)
-    group = (row >= 160).astype(jnp.int32) + (row >= 320).astype(jnp.int32) + (row >= 480).astype(jnp.int32)
-    rem = row - 160 * group
-    step20 = jnp.zeros_like(rem)
-    for t in range(1, NZ):
-        step20 = step20 + (rem >= PIECE * t).astype(jnp.int32)
-    wanted = ROWS * step20 + PIECE * group + rem - PIECE * step20
-    perm[...] = jnp.where(col == wanted, 1.0, 0.0).astype(BF16)
-
-    def gathered_order(v):
-        return dot(v, perm[...]).astype(BF16)
-
-    loads[3].wait()
-    kbuf[OWN] = gathered_order(kin[...])
     pl.semaphore_wait(barrier, 12 - jnp.where(own_w, 1, 0))
 
     k_w = ids(4)
@@ -155,6 +140,22 @@
                 def _():
                     lc.start()
                     lc.wait()
+
+    row = lax.broadcasted_iota(jnp.int32, (DC, DC), 0)
+    col = lax.broadcasted_iota(jnp.int32, (DC, DC), 1)
+    group = (row >= 160).astype(jnp.int32) + (row >= 320).astype(jnp.int32) + (row >= 480).astype(jnp.int32)
+    rem = row - 160 * group
+    step20 = jnp.zeros_like(rem)
+    for t in range(1, NZ):
+        step20 = step20 + (rem >= PIECE * t).astype(jnp.int32)
+    wanted = ROWS * step20 + PIECE * group + rem - PIECE * step20
+    perm[...] = jnp.where(col == wanted, 1.0, 0.0).astype(BF16)
+
+    def gathered_order(v):
+        return dot(v, perm[...]).astype(BF16)
+
+    loads[3].wait()
+    kbuf[OWN] = gathered_order(kin[...])
 
     def x_out(buf, k):
         send(buf.at[OWN], buf.at[LEFT], k, xr)

time: 87.1 us -> 87.2 us (level)
  no operation moved by 1% of the time
where the time goes in v7:
time: 87.2 us; the launch traced here: 87.1 us
  Pallas kernels  85.4 us (98%)
  local copies, waits for them, and re-layouts  1.66 us (2%)
    pallas_call x1, Pallas kernels, body(): pl.pallas_call(kernel, out_shape=jax.ShapeDtypeStruct((TOK, DC), BF16), i...  85.4 us

profile of v7, /device:TPU:1, one launch (start us, length us, event | category | flops | bytes accessed | tf_op | source)
XLA Modules:
  0.0 87.1 jit_solution(5819554220578845668)
XLA Ops:
  0.0 85.4 %ttt_layer.1 = bf16[192,640]{1,0:T(8,128)(2,1)} custom-call(bf16[192,640]{1,0:T(8,128)(2,1)} %k_hbm.1, bf16[192,640]{1,0:T(8,128)(2,1)} %v_hbm.1, bf16[192,640]{1,0:T(8,128)(2,1)} %q_hbm.1, f32[2,192]{1,0:T(2,128)} %bitcast.1, bf16[20,768]{1,0:T(8,128)(2,1)} %w1_hbm.1, bf16[20,768]{1,0:T(8,128)(2,1)} %w3_hbm.1, bf16[20,768]{1,0:T(8,128)(2,1)} %w2_hbm.1), custom_call_target="tpu_custom_call" | custom-call | tf_op jit(solution)/shard_map/ttt_layer/pallas_call | solution.py:470
  85.5 1.7 %copy.9 = bf16[192,640]{1,0:T(8,128)(2,1)} copy(bf16[192,640]{1,0:T(8,128)(2,1)} %ttt_layer.1) | data formatting | bytes 491520

commit v8 on v6

--- a/solution.py
+++ b/solution.py
@@ -409,6 +409,8 @@
     sms[4:5, :] = square_sums(nw[:, 1].reshape(DC, U))
     send(sms, smr, k_s, peer)
     q_part(LEFT, 1)
+    q_part(RIGHT, 1)
+    q_part(OWN, 1)
     arrived(smr, k_s, peer)
     sums = sms[...] + smr[...]
     ra, rb, r2 = [jnp.sqrt((sums[m:m + 1] + EPS) / (sums[3 + m:4 + m] + EPS)) for m in range(3)]
@@ -432,12 +434,10 @@
     ob[OPP] = part.astype(BF16)
     send(ob.at[OPP, 0:HALF], obr.at[0:HALF], k_x, xr)
     send(ob.at[OPP, HALF:TOK], obr.at[HALF:TOK], k_x + 1, xl)
-    q_part(RIGHT, 1)
     part = out_part(LEFT)
     ob[LEFT, 0:HALF] = part[0:HALF].astype(BF16)
     send(ob.at[LEFT, 0:HALF], fin.at[1, 0:HALF], k_x + 2, xl)
     op[0] = part[HALF:TOK]
-    q_part(OWN, 1)
     part = out_part(RIGHT)
     ob[RIGHT, HALF:TOK] = part[HALF:TOK].astype(BF16)
     send(ob.at[RIGHT, HALF:TOK], fin.at[0, HALF:TOK], k_x + 4, xr)

time: 87.1 us -> 87.1 us (level)
  no operation moved by 1% of the time
where the time goes in v8:
time: 87.1 us; the launch traced here: 87 us
  Pallas kernels  85.4 us (98%)
  local copies, waits for them, and re-layouts  1.66 us (2%)
    pallas_call x1, Pallas kernels, body(): pl.pallas_call(kernel, out_shape=jax.ShapeDtypeStruct((TOK, DC), BF16), i...  85.4 us

profile of v8, /device:TPU:1, one launch (start us, length us, event | category | flops | bytes accessed | tf_op | source)
XLA Modules:
  0.0 87.0 jit_solution(5332456605826363151)
XLA Ops:
  0.0 85.4 %ttt_layer.1 = bf16[192,640]{1,0:T(8,128)(2,1)} custom-call(bf16[192,640]{1,0:T(8,128)(2,1)} %k_hbm.1, bf16[192,640]{1,0:T(8,128)(2,1)} %v_hbm.1, bf16[192,640]{1,0:T(8,128)(2,1)} %q_hbm.1, f32[2,192]{1,0:T(2,128)} %bitcast.1, bf16[20,768]{1,0:T(8,128)(2,1)} %w1_hbm.1, bf16[20,768]{1,0:T(8,128)(2,1)} %w3_hbm.1, bf16[20,768]{1,0:T(8,128)(2,1)} %w2_hbm.1), custom_call_target="tpu_custom_call" | custom-call | tf_op jit(solution)/shard_map/ttt_layer/pallas_call | solution.py:469
  85.4 1.7 %copy.9 = bf16[192,640]{1,0:T(8,128)(2,1)} copy(bf16[192,640]{1,0:T(8,128)(2,1)} %ttt_layer.1) | data formatting | bytes 491520
